TPU v7x, 32 devices: a whole 2x2x4 slice. The times are simulated.
32 devices in a mesh: cohort: 2 (over y), bx: 16 (over z, x, core).
Axes of the slice: x: 2, y: 2, z: 4, core: 2. Of those that a mesh axis runs over, the one named last changes fastest.
Arguments:
- bold: bfloat16 [256, 12, 4096], P('cohort', None, 'bx'), parts along dimension 0, may hold values from -6 to 6
- nbr_table: int32 [256, 4096], P('cohort', 'bx'), parts along dimension 0, may hold values from -1 to 767, as said below
- subject: int32 [256], P('cohort'), parts along dimension 0, may hold values from 0 to 7
Outputs:
- spread: float32 [8192], P(('cohort', 'bx')), parts along dimension 0
- gram_mean: float32 [256, 128], P('cohort'), parts along dimension 0
There are 2 independent parts, one for each index of `cohort`. A program takes and returns all parts, laid end to end along the dimension named above; each array names one. Nothing has to cross between parts.
Inputs may be any that keep to these rules, and one draw needn't show every extreme that they name: `nbr_table`: rows 125 to 127 are all -1 and row (124) // 2 names the centre itself (256 + its place in its block). Any other entry is -1 or the place, in the window made of the previous block, the centre's own block and the next block (768 voxels in order), of a voxel at most 147 voxels away from the centre in voxel order; no entry names a voxel outside the cohort's 4096 voxels.
All inputs are finite; a program needn't handle non-finite values.
Results may differ from a plain program's by a relative error of at most 0.0003.
Values may be sent and summed in bfloat16 or wider, within the bound.
A program may use at most 64 MiB of HBM per device.

v0:
```python
import functools

import jax
import jax.numpy as jnp
from jax import lax
from jax.experimental import pallas as pl
from jax.experimental.pallas import tpu as pltpu
from jax.sharding import PartitionSpec as P

NB = 125
SUBJ = 8
REACH = 147
VARIANCE_FLOOR = 0.05

SLOTS = 16
GROUP = 16
CHUNK = 64
LANES = 128
LEAD = 160
SPAN = 384
BATCH = 4
MESH = pl.DeviceIdType.MESH
BY_ROW = lax.GatherDimensionNumbers(
    offset_dims=(), collapsed_slice_dims=(0,), start_index_map=(0,),
    operand_batching_dims=(1,), start_indices_batching_dims=(1,))


def normalized(raw):
    values = raw.astype(jnp.float32)
    points = values.shape[0]
    centred = values - jnp.sum(values, axis=0, keepdims=True) * (1.0 / points)
    return centred * (1.0 / jnp.sqrt(jnp.sum(centred * centred, axis=0, keepdims=True) + 1.0))


def prepare_kernel(idx_ref, bold_ref, root_ref, own_ref, hit_ref):
    slots, block_len = idx_ref.shape
    points, epochs, _ = bold_ref.shape
    depth = GROUP * SLOTS
    for half in range(block_len // LANES):
        place = lax.broadcasted_iota(jnp.int32, (1, LANES), 1) + half * LANES
        shift = block_len - LEAD + place // CHUNK * CHUNK

        def one_tile(w, carry):
            at = lax.broadcasted_iota(jnp.int32, (32, LANES), 0) + w * 32 + shift
            hits = jnp.zeros((32, LANES), jnp.float32)
            for j in range(NB):
                named = idx_ref[j:j + 1, half * LANES:(half + 1) * LANES]
                hits = jnp.where(jnp.broadcast_to(named, (32, LANES)) == at, hits + 1.0, hits)
            hit_ref[pl.ds(pl.multiple_of(w * 32, 32), 32), :] = jnp.sqrt(hits)
            return carry

        lax.fori_loop(0, SPAN // 32, one_tile, 0)
        for t in range(SPAN // LANES):
            root_ref[half * LANES:(half + 1) * LANES, t * LANES:(t + 1) * LANES] = (
                hit_ref[t * LANES:(t + 1) * LANES, :].T)

    def one_group(g, carry):
        rows = pl.ds(pl.multiple_of(g * GROUP, GROUP), GROUP)
        rounded = normalized(bold_ref[:, rows, :]).astype(jnp.bfloat16).astype(jnp.float32)
        flat = rounded.reshape(points * GROUP, block_len)
        flat = jnp.concatenate([flat, jnp.zeros((depth - points * GROUP, block_len), jnp.float32)], axis=0)
        own_ref[:, pl.ds(pl.multiple_of(g * depth, depth), depth)] = flat.T
        return carry

    lax.fori_loop(0, epochs // GROUP, one_group, 0)


def features_kernel(ext_ref, own_ref, root_ref, sid_ref, hot_ref, inv_ref, keep_ref,
                    square_ref, gram_ref, win_ref, lhs_ref, prod_ref, mean_ref, sq_ref, feat_ref, var_ref):
    chunk = pl.program_id(0)
    first = chunk * CHUNK
    parity = lax.rem(chunk, 2)
    start = pl.multiple_of((chunk // 2) * LANES, LANES)
    epochs = gram_ref.shape[0]
    depth = GROUP * SLOTS
    groups = epochs // GROUP

    row_epoch = lax.broadcasted_iota(jnp.int32, (GROUP, depth), 0)
    col_epoch = lax.broadcasted_iota(jnp.int32, (GROUP, depth), 1) % GROUP
    diagonal = row_epoch == col_epoch

    @pl.when(chunk == 0)
    def _():
        gram_ref[...] = jnp.zeros_like(gram_ref)
        points = ext_ref.shape[0]
        wide = win_ref.shape[2]
        filler = jnp.zeros((depth - points * GROUP, wide), jnp.bfloat16)

        def fill(g, carry):
            rows = pl.ds(pl.multiple_of(g * GROUP, GROUP), GROUP)
            cells = normalized(ext_ref[:, rows, :]).reshape(points * GROUP, -1)
            base = pl.multiple_of(g * depth, depth)
            for side in range(2):
                win_ref[side, pl.ds(base, points * GROUP), :] = (
                    cells[:, side * CHUNK:side * CHUNK + wide].astype(jnp.bfloat16))
                win_ref[side, pl.ds(base + points * GROUP, depth - points * GROUP), :] = filler
            return carry

        lax.fori_loop(0, groups, fill, 0)

    def one_group(g, carry):
        cols = pl.ds(pl.multiple_of(g * depth, depth), depth)
        for c in range(CHUNK):
            row = jnp.broadcast_to(own_ref[pl.ds(first + c, 1), cols], (GROUP, depth))
            lhs_ref[c * GROUP:(c + 1) * GROUP, :] = jnp.where(diagonal, row, 0.0).astype(jnp.bfloat16)
        prod = jnp.dot(lhs_ref[...], win_ref[parity, cols, pl.ds(start, SPAN)],
                       preferred_element_type=jnp.float32)
        prod_ref[:, pl.ds(pl.multiple_of(g * GROUP, GROUP), GROUP), :] = prod.reshape(CHUNK, GROUP, SPAN)
        for c in range(CHUNK // 2):
            pair = []
            for i in range(2):
                row = jnp.broadcast_to(own_ref[pl.ds(first + 2 * c + i, 1), cols], (SUBJ, depth))
                pair.append(row * keep_ref[:, cols])
            lhs_ref[c * GROUP:(c + 1) * GROUP, :] = jnp.concatenate(pair, axis=0).astype(jnp.bfloat16)
        part = jnp.dot(lhs_ref[:CHUNK * SUBJ, :], win_ref[parity, cols, pl.ds(start, SPAN)],
                       preferred_element_type=jnp.float32).reshape(CHUNK, SUBJ, SPAN)

        @pl.when(g == 0)
        def _():
            mean_ref[...] = part

        @pl.when(g > 0)
        def _():
            mean_ref[...] += part
        return carry

    lax.fori_loop(0, groups, one_group, 0)

    inv = jnp.concatenate([inv_ref[...]] * (SPAN // LANES), axis=1)
    feat_ref[...] = jnp.zeros_like(feat_ref)
    steps = CHUNK // BATCH

    def expand(stat, r):
        at = sid_ref[r * 8:(r + 1) * 8, :]
        return jnp.concatenate(
            [lax.gather(stat[:, t * LANES:(t + 1) * LANES], at[..., None], BY_ROW, (1, 1),
                        mode="promise_in_bounds")
             for t in range(SPAN // LANES)], axis=1)

    def one_batch(p, carry):
        base_c = jnp.maximum(p - 2, 0) * BATCH
        base_b = jnp.clip(p - 1, 0, steps - 1) * BATCH
        base_a = jnp.minimum(p, steps - 1) * BATCH
        total = None
        for i in range(BATCH):
            feat = feat_ref[i]
            kern = lax.dot_general(feat, feat, (((1,), (1,)), ((), ())), preferred_element_type=jnp.float32)
            square_ref[pl.ds(first + base_c + i, 1), :] = jnp.sum(kern * kern, axis=0, keepdims=True)
            total = kern if total is None else total + kern
        gram_ref[...] += total
        for i in range(BATCH):
            scale = lax.rsqrt(var_ref[i] * inv + VARIANCE_FLOOR) * root_ref[pl.ds(first + base_b + i, 1), :]
            scale = jnp.where(p > 0, scale, 0.0)
            for r in range(0, epochs // 8, 2):
                pair = [prod_ref[base_b + i, (r + k) * 8:(r + k + 1) * 8, :] * expand(scale, r + k) for k in range(2)]
                feat_ref[i, r * 8:(r + 2) * 8, :] = jnp.concatenate(pair, axis=0).astype(jnp.bfloat16)
        for i in range(BATCH):
            mean = mean_ref[base_a + i] * inv
            for r in range(0, epochs // 8, 2):
                pair = []
                for k in range(2):
                    rows = slice((r + k) * 8, (r + k + 1) * 8)
                    dev = prod_ref[base_a + i, rows, :] - expand(mean, r + k)
                    prod_ref[base_a + i, rows, :] = dev
                    pair.append(dev * dev)
                sq_ref[i, r * 8:(r + 2) * 8, :] = jnp.concatenate(pair, axis=0).astype(jnp.bfloat16)
            var_ref[i] = jnp.dot(hot_ref[...], sq_ref[i], preferred_element_type=jnp.float32)[:SUBJ]
        return carry

    lax.fori_loop(0, steps + 2, one_batch, 0)


def sum_kernel(count, scale, part_ref, out_ref, took, send1, recv1, send2, recv2):
    me = lax.axis_index("bx")
    barrier = pltpu.get_barrier_semaphore()

    def greet(d, carry):
        pl.semaphore_signal(barrier, inc=1, device_id={"bx": lax.rem(me + d, count)}, device_id_type=MESH)
        return carry

    lax.fori_loop(1, count, greet, 0)
    pl.semaphore_wait(barrier, count - 1)

    def scatter(d):
        to = lax.rem(me + d, count)
        return pltpu.make_async_remote_copy(
            src_ref=part_ref.at[to], dst_ref=took.at[d], send_sem=send1.at[d], recv_sem=recv1.at[d],
            device_id={"bx": to}, device_id_type=MESH)

    def gather(d):
        return pltpu.make_async_remote_copy(
            src_ref=out_ref.at[me], dst_ref=out_ref.at[me], send_sem=send2.at[d], recv_sem=recv2.at[d],
            device_id={"bx": lax.rem(me + d, count)}, device_id_type=MESH)

    def landed(d):
        src = lax.rem(me + count - d, count)
        return pltpu.make_async_remote_copy(
            src_ref=out_ref.at[src], dst_ref=out_ref.at[src], send_sem=send2.at[d], recv_sem=recv2.at[d],
            device_id={"bx": lax.rem(me + d, count)}, device_id_type=MESH)

    def each(act):
        def body(d, carry):
            act(d)
            return carry
        lax.fori_loop(1, count, body, 0)

    each(lambda d: scatter(d).start())
    each(lambda d: scatter(d).wait_recv())

    def add(d, total):
        return total + took[d]

    out_ref[me] = lax.fori_loop(1, count, add, part_ref[me]) * scale
    each(lambda d: gather(d).start())
    each(lambda d: landed(d).wait_recv())
    each(lambda d: scatter(d).wait_send())
    each(lambda d: gather(d).wait_send())


def sum_over_bx(total, scale):
    count = lax.axis_size("bx")
    rows, cols = total.shape
    blocks = total.reshape(count, rows // count, cols)
    vmem = pl.BlockSpec(memory_space=pltpu.VMEM)
    return pl.pallas_call(
        functools.partial(sum_kernel, count, scale),
        in_specs=[vmem],
        out_specs=vmem,
        out_shape=jax.ShapeDtypeStruct(blocks.shape, jnp.float32),
        scratch_shapes=[pltpu.VMEM(blocks.shape, jnp.float32)] + [pltpu.SemaphoreType.DMA((count,))] * 4,
        compiler_params=pltpu.CompilerParams(collective_id=0, has_side_effects=True),
        name="sum_over_bx",
    )(blocks).reshape(rows, cols)


def per_device(bold, nbr_table, subject):
    epochs, points, block_len = bold.shape
    count = lax.axis_size("bx")
    bold = bold.transpose(1, 0, 2)
    left = lax.ppermute(bold[:, :, block_len - LEAD:], "bx", [(i, i + 1) for i in range(count - 1)])
    right = lax.ppermute(bold[:, :, :LEAD], "bx", [(i + 1, i) for i in range(count - 1)])
    vmem = pl.BlockSpec(memory_space=pltpu.VMEM)
    wide = SPAN + LANES
    depth = GROUP * SLOTS
    span = epochs * SLOTS
    root, own = pl.pallas_call(
        prepare_kernel,
        in_specs=[vmem] * 2,
        out_specs=[vmem] * 2,
        out_shape=[jax.ShapeDtypeStruct((block_len, SPAN), jnp.float32),
                   jax.ShapeDtypeStruct((block_len, span), jnp.float32)],
        scratch_shapes=[pltpu.VMEM((SPAN, LANES), jnp.float32)],
        cost_estimate=pl.CostEstimate(flops=2 * 10 ** 9, bytes_accessed=4 * 10 ** 6, transcendentals=0),
        name="prepare",
    )(nbr_table, bold)
    ext = jnp.concatenate([left, bold, right], axis=2)
    onehot = subject[None, :] == jnp.arange(SUBJ, dtype=jnp.int32)[:, None]
    counts = jnp.maximum(jnp.sum(onehot.astype(jnp.float32), axis=1), 1.0)
    inv = jnp.broadcast_to((1.0 / counts)[:, None], (SUBJ, LANES))
    sid = jnp.broadcast_to(subject[:, None], (epochs, LANES))
    hot = jnp.pad(onehot.astype(jnp.bfloat16), ((0, 8), (0, 0)))
    keep = jnp.broadcast_to(onehot.astype(jnp.float32).reshape(SUBJ, -1, 1, GROUP),
                            (SUBJ, epochs // GROUP, SLOTS, GROUP)).reshape(SUBJ, span)
    squares, total = pl.pallas_call(
        features_kernel,
        grid=(block_len // CHUNK,),
        in_specs=[vmem] * 7,
        out_specs=[vmem] * 2,
        out_shape=[jax.ShapeDtypeStruct((block_len, epochs), jnp.float32),
                   jax.ShapeDtypeStruct((epochs, epochs), jnp.float32)],
        scratch_shapes=[
            pltpu.VMEM((2, span, wide), jnp.bfloat16),
            pltpu.VMEM((CHUNK * GROUP, depth), jnp.bfloat16),
            pltpu.VMEM((CHUNK, epochs, SPAN), jnp.float32),
            pltpu.VMEM((CHUNK, SUBJ, SPAN), jnp.float32),
            pltpu.VMEM((BATCH, epochs, SPAN), jnp.bfloat16),
            pltpu.VMEM((BATCH, epochs, SPAN), jnp.bfloat16),
            pltpu.VMEM((BATCH, SUBJ, SPAN), jnp.float32),
        ],
        compiler_params=pltpu.CompilerParams(dimension_semantics=("arbitrary",),
                                             vmem_limit_bytes=60 * 1024 * 1024),
        name="features",
    )(ext, own, root, sid, hot, inv, keep)
    spread = jnp.sqrt(jnp.sum(squares, axis=1) / (epochs * NB * NB))
    gram_mean = sum_over_bx(total, 1.0 / (NB * block_len * count))
    return spread, gram_mean


def solution(mesh):
    return jax.shard_map(
        per_device,
        mesh=mesh,
        in_specs=(P("cohort", None, "bx"), P("cohort", "bx"), P("cohort")),
        out_specs=(P(("cohort", "bx")), P("cohort", None)),
        check_vma=False,
    )
```

profile of v0, /device:TPU:0, one launch (start us, length us, event | category | flops | bytes accessed | tf_op | source)
XLA Modules:
  0.0 106.2 jit_solution(6007765167040136051)
XLA Ops:
  0.6 0.0 copy-start.1
  0.6 1.9 %fusion.1 = (bf16[12,128,160]{2,1,0:T(8,128)(2,1)S(1)}, bf16[12,128,160]{2,1,0:T(8,128)(2,1)S(1)}) fusion(bf16[12,128,256]{2,1,0:T(8,128)(2,1)} %bitcast.5), kind=kLoop, calls=%fused_computation.8 | loop fusion | bytes 1966080 | tf_op jit(solution)/shard_map/slice | solution.py:240
  2.6 0.3 copy.6
  2.9 1.3 %collective-permute-start.1 = (bf16[12,128,160]{1,2,0:T(8,128)(2,1)S(1)}, bf16[12,128,160]{1,2,0:T(8,128)(2,1)S(1)}, u32[]{:S(2)}, u32[]{:S(2)}) collective-permute-start(bf16[12,128,160]{1,2,0:T(8,128)(2,1)S(1)} %copy.6), channel_id=1, source_target_pairs={{1,0},{2,1},{3,2},{4,3},{5,4},{6,5},{7,6},{8,7},{9,8},{10,9},{11,1... | collective-permute-start | bytes 1474568 | tf_op jit(solution)/shard_map/ppermute | solution.py:241
  4.2 0.3 copy.5
  4.6 3.1 %collective-permute-start = (bf16[12,128,160]{1,2,0:T(8,128)(2,1)S(1)}, bf16[12,128,160]{1,2,0:T(8,128)(2,1)S(1)}, u32[]{:S(2)}, u32[]{:S(2)}) collective-permute-start(bf16[12,128,160]{1,2,0:T(8,128)(2,1)S(1)} %copy.5), channel_id=1, source_target_pairs={{0,1},{1,2},{2,3},{3,4},{4,5},{5,6},{6,7},{7,8},{8,9},{9,10},{10,1... | collective-permute-start | bytes 1474568 | tf_op jit(solution)/shard_map/ppermute | solution.py:240
  7.7 0.1 eq.28
  7.8 0.6 pad_convert_fusion.hot_ref
  8.4 0.9 reshape.33.keep_ref
  9.3 0.1 convert_reduce_fusion
  9.4 11.2 %prepare.1 = (f32[256,384]{1,0:T(8,128)}, f32[256,2048]{1,0:T(8,128)}) custom-call(s32[128,256]{1,0:T(8,128)} %idx_ref.1, bf16[12,128,256]{2,1,0:T(8,128)(2,1)} %bitcast.6), custom_call_target="tpu_custom_call" | custom-call | flops 2000000000 | bytes 4000000 | tf_op jit(solution)/shard_map/prepare/pallas_call | solution.py:246
  20.6 0.0 collective-permute-done.1
  20.6 0.3 copy.8
  20.9 0.0 collective-permute-done
  20.9 0.3 copy.7
  21.2 0.5 copy-done
  21.7 2.2 %pad_maximum_fusion.ext_ref = bf16[12,128,576]{2,1,0:T(8,128)(2,1)} fusion(bf16[12,128,160]{2,1,0:T(8,128)(2,1)S(1)} %copy.8, bf16[12,128,256]{2,1,0:T(8,128)(2,1)S(1)} %bitcast.7, bf16[12,128,160]{2,1,0:T(8,128)(2,1)S(1)} %copy.7), kind=kLoop, calls=%fused_computation | loop fusion | flops 5308416 | bytes 3538944 | tf_op jit(solution)/shard_map/concatenate | solution.py:256
  23.9 0.7 broadcast_in_dim.7.inv_ref
  24.6 0.7 broadcast_in_dim.6.sid_ref
  25.3 60.7 %features.1 = (f32[256,128]{1,0:T(8,128)}, f32[128,128]{1,0:T(8,128)}) custom-call(bf16[12,128,576]{2,1,0:T(8,128)(2,1)} %pad_maximum_fusion.ext_ref, f32[256,2048]{1,0:T(8,128)} %get-tuple-element.6.own_ref, f32[256,384]{1,0:T(8,128)} %get-tuple-element.7.root_ref, s32[128,128]{1,0:T(8,128)} %broadcast_in_dim.6.sid_ref, ...), custom_call_target="tpu_custom_call" | custom-call | tf_op jit(solution)/shard_map/features/pallas_call | solution.py:264
  85.9 1.0 reduce_sum.19
  86.9 0.6 multiply_sqrt_fusion
  87.5 17.2 %sum_over_bx.1 = f32[16,8,128]{2,1,0:T(8,128)} custom-call(f32[16,8,128]{2,1,0:T(8,128)} %bitcast.9), custom_call_target="tpu_custom_call" | custom-call | tf_op jit(solution)/shard_map/sum_over_bx/pallas_call | solution.py:225
  104.7 1.5 %copy.10 = f32[128,128]{1,0:T(8,128)} copy(f32[128,128]{1,0:T(8,128)} %bitcast.8) | data formatting | bytes 131072
  (6 shorter events, 0.1 us)
Async XLA Ops:
  0.6 7.0 %copy-start.1 = (s32[128]{0:T(128)S(1)}, s32[128]{0:T(128)}, u32[]{:S(2)}) copy-start(s32[128]{0:T(128)} %param.5) | copy-start | bytes 1540
  2.9 17.6 %collective-permute-start.1 = (bf16[12,128,160]{1,2,0:T(8,128)(2,1)S(1)}, bf16[12,128,160]{1,2,0:T(8,128)(2,1)S(1)}, u32[]{:S(2)}, u32[]{:S(2)}) collective-permute-start(bf16[12,128,160]{1,2,0:T(8,128)(2,1)S(1)} %copy.6), channel_id=1, source_target_pairs={{1,0},{2,1},{3,2},{4,3},{5,4},{6,5},{7,6},{8,7},{9,8},{10,9},{11,1... | collective-permute-start | bytes 1474568 | tf_op jit(solution)/shard_map/ppermute | solution.py:241
  4.6 16.3 %collective-permute-start = (bf16[12,128,160]{1,2,0:T(8,128)(2,1)S(1)}, bf16[12,128,160]{1,2,0:T(8,128)(2,1)S(1)}, u32[]{:S(2)}, u32[]{:S(2)}) collective-permute-start(bf16[12,128,160]{1,2,0:T(8,128)(2,1)S(1)} %copy.5), channel_id=1, source_target_pairs={{0,1},{1,2},{2,3},{3,4},{4,5},{5,6},{6,7},{7,8},{8,9},{9,10},{10,1... | collective-permute-start | bytes 1474568 | tf_op jit(solution)/shard_map/ppermute | solution.py:240
  20.6 1.1 %copy-start = (bf16[128,12,256]{2,0,1:T(8,128)(2,1)S(1)}, bf16[128,12,256]{2,0,1:T(8,128)(2,1)}, u32[]{:S(2)}) copy-start(bf16[128,12,256]{2,0,1:T(8,128)(2,1)} %param.3) | copy-start | bytes 2359300
where the time goes:
time: 107 us; the launch traced here: 106 us
  Pallas kernels  89 us (83%)
  local copies, waits for them, and re-layouts  7.59 us (7%)
  other arithmetic  4.51 us (4%)
  starting transfers between devices  4.35 us (4%)
    pallas_call x1, Pallas kernels, per_device(): pl.pallas_call(features_kernel, grid=(block_len // CHUNK,), in_specs=[vme...  60.7 us
    pallas_call x1, Pallas kernels, sum_over_bx(): pl.pallas_call(functools.partial(sum_kernel, count, scale), in_specs=[vme...  17.2 us
    pallas_call x1, Pallas kernels, per_device(): pl.pallas_call(prepare_kernel, in_specs=[vmem] * 2, out_specs=[vmem] * 2,...  11.2 us
    ppermute x1, starting transfers between devices, per_device(): lax.ppermute(bold[:, :, block_len - LEAD:], 'bx', [(i, i + 1) for i in ra...  3.06 us
    slice x2, local copies, waits for them, and re-layouts, per_device(): bold[:, :, block_len - LEAD:]  2.3 us
    concatenate x1, other arithmetic, per_device(): ext = jnp.concatenate([left, bold, right], axis=2)  2.2 us
  transfers between devices with their start and end apart: 2, of which 0 were waited for; matrix products, arithmetic and copies ran while one was open for 2% of the time, Pallas kernels for 11%

commit v1 on v0

v1 whole, which is shorter than its diff:
```python
import functools

import jax
import jax.numpy as jnp
from jax import lax
from jax.experimental import pallas as pl
from jax.experimental.pallas import tpu as pltpu
from jax.sharding import PartitionSpec as P

NB = 125
SUBJ = 8
REACH = 147
VARIANCE_FLOOR = 0.05

LANES = 128
ROWS = 8
GROUP = 8
CHUNK = 64
LEAD = 160
SPAN = 384
MESH = pl.DeviceIdType.MESH
BY_ROW = lax.GatherDimensionNumbers(
    offset_dims=(), collapsed_slice_dims=(0,), start_index_map=(0,),
    operand_batching_dims=(1,), start_indices_batching_dims=(1,))
BY_LANE = lax.GatherDimensionNumbers(
    offset_dims=(), collapsed_slice_dims=(1,), start_index_map=(1,),
    operand_batching_dims=(0,), start_indices_batching_dims=(0,))


def take(values, at, dims):
    return lax.gather(values, at[..., None], dims, (1, 1), mode="promise_in_bounds")


def normalized(values):
    points = values.shape[0]
    centred = values - jnp.sum(values, axis=0, keepdims=True) * (1.0 / points)
    return centred * (1.0 / jnp.sqrt(jnp.sum(centred * centred, axis=0, keepdims=True) + 1.0))


def features_kernel(ext_ref, idx_ref, subject_ref, spread_ref, gram_ref,
                    sorted_ref, win_ref, own_ref, lane_ref, tile_ref, valid_ref, sid_ref, perm_ref,
                    x0_ref, x1_ref, sum0_ref, sum1_ref, sq0_ref, sq1_ref, mean0_ref, mean1_ref,
                    scale0_ref, scale1_ref, square_ref, total_ref):
    points, epochs, wide = ext_ref.shape
    slots, block_len = idx_ref.shape
    groups = epochs // GROUP
    depth = points * GROUP
    span = SPAN + LANES

    named = jnp.broadcast_to(subject_ref[...], (epochs, LANES))
    named_t = named.T
    row = lax.broadcasted_iota(jnp.int32, (epochs, LANES), 0)
    col = lax.broadcasted_iota(jnp.int32, (epochs, LANES), 1)
    ahead = (named_t < named) | ((named_t == named) & (row < col))
    rank = jnp.sum(ahead.astype(jnp.float32), axis=0, keepdims=True).astype(jnp.int32)
    perm = (jnp.broadcast_to(rank, (epochs, LANES)) == row).astype(jnp.float32)
    perm_ref[...] = perm
    perm16 = perm.astype(jnp.bfloat16)
    one_row = subject_ref[...]
    starts = [jnp.sum((one_row < s).astype(jnp.float32)).astype(jnp.int32) for s in range(SUBJ + 1)]
    place = lax.broadcasted_iota(jnp.int32, (epochs, LANES), 0)
    sid = jnp.zeros((epochs, LANES), jnp.int32)
    for s in range(1, SUBJ):
        sid = sid + (place >= starts[s]).astype(jnp.int32)
    sid_ref[...] = sid

    def arrange(t, carry):
        sorted_ref[t] = jnp.dot(perm16, ext_ref[t], preferred_element_type=jnp.float32)
        return carry

    lax.fori_loop(0, points, arrange, 0)

    blank = jnp.zeros((LANES - depth, block_len), jnp.float32)

    def fill(g, carry):
        cells = normalized(sorted_ref[:, pl.ds(pl.multiple_of(g * GROUP, GROUP), GROUP), :])
        cells = cells.reshape(depth, wide)
        base = pl.multiple_of(g * depth, depth)
        for side in range(2):
            win_ref[side, pl.ds(base, depth), :] = cells[:, side * CHUNK:side * CHUNK + span].astype(jnp.bfloat16)
        own = cells[:, LEAD:LEAD + block_len].astype(jnp.bfloat16).astype(jnp.float32)
        flat = jnp.concatenate([own, blank], axis=0).T
        for b in range(block_len // ROWS):
            piece = flat[b * ROWS:(b + 1) * ROWS, :]
            own_ref[b, g] = jnp.concatenate([piece, piece], axis=0).astype(jnp.bfloat16)
        return carry

    lax.fori_loop(0, groups, fill, 0)

    for half in range(block_len // LANES):
        at = idx_ref[:, half * LANES:(half + 1) * LANES].T
        centre = lax.broadcasted_iota(jnp.int32, (LANES, slots), 0) + half * LANES
        offset = at - (block_len - LEAD) - centre // CHUNK * CHUNK
        part = slice(half * LANES, (half + 1) * LANES)
        valid_ref[part, :] = (at >= 0).astype(jnp.float32)
        lane_ref[part, :] = jnp.where(at >= 0, offset & (LANES - 1), 0)
        tile_ref[part, :] = jnp.where(at >= 0, offset >> 7, 0)

    total_ref[...] = jnp.zeros_like(total_ref)
    masks = []
    for p in range(GROUP // 2):
        which = lax.broadcasted_iota(jnp.int32, (2 * ROWS, LANES), 0) // ROWS + 2 * p
        lane = lax.broadcasted_iota(jnp.int32, (2 * ROWS, LANES), 1) % GROUP
        masks.append((which == lane).astype(jnp.float32).astype(jnp.bfloat16))
    inverse = [1.0 / jnp.maximum((starts[s + 1] - starts[s]).astype(jnp.float32), 1.0) for s in range(SUBJ)]
    for sum_ref, sq_ref in ((sum0_ref, sq0_ref), (sum1_ref, sq1_ref)):
        sum_ref[0] = jnp.zeros((ROWS, LANES), jnp.float32)
        sq_ref[0] = jnp.zeros((ROWS, LANES), jnp.float32)

    def correlate(b, refs):
        x_ref, sum_ref, sq_ref = refs[:3]
        chunk = b // (CHUNK // ROWS)
        start = pl.multiple_of((chunk // 2) * LANES, LANES)
        here = pl.ds(pl.multiple_of(b * ROWS, ROWS), ROWS)
        lane = lane_ref[here, :]
        tile = tile_ref[here, :]
        first = tile == 0
        second = tile == 1
        running = jnp.zeros((ROWS, LANES), jnp.float32)
        squares = jnp.zeros((ROWS, LANES), jnp.float32)
        for g in range(groups):
            rhs = win_ref[lax.rem(chunk, 2), g * depth:(g + 1) * depth, pl.ds(start, SPAN)]
            own = own_ref[b, g]
            lhs = jnp.concatenate([own * m for m in masks], axis=0)[:, :depth]
            prod = jnp.dot(lhs, rhs, preferred_element_type=jnp.float32)
            for e in range(GROUP):
                r = e * ROWS
                parts = [take(prod[r:r + ROWS, t * LANES:(t + 1) * LANES], lane, BY_LANE)
                         for t in range(SPAN // LANES)]
                x = jnp.where(first, parts[0], jnp.where(second, parts[1], parts[2]))
                i = g * GROUP + e
                x_ref[i * ROWS:(i + 1) * ROWS, :] = x
                running = running + x
                squares = squares + x * x
                sum_ref[i + 1] = running
                sq_ref[i + 1] = squares

    def kernels(b, refs):
        x_ref, sum_ref, sq_ref, mean_ref, scale_ref = refs
        valid = valid_ref[pl.ds(pl.multiple_of(b * ROWS, ROWS), ROWS), :]
        for s in range(SUBJ):
            mean = (sum_ref[starts[s + 1]] - sum_ref[starts[s]]) * inverse[s]
            second = (sq_ref[starts[s + 1]] - sq_ref[starts[s]]) * inverse[s]
            var = jnp.maximum(second - mean * mean, 0.0)
            mean_ref[s * ROWS:(s + 1) * ROWS, :] = mean
            scale_ref[s * ROWS:(s + 1) * ROWS, :] = lax.rsqrt(var + VARIANCE_FLOOR) * valid
        acc = None
        for r in range(ROWS):
            mean = mean_ref[pl.ds(r, SUBJ, stride=ROWS), :]
            scale = scale_ref[pl.ds(r, SUBJ, stride=ROWS), :]
            pieces = []
            for q in range(epochs // 8):
                at = sid_ref[q * 8:(q + 1) * 8, :]
                x = x_ref[pl.ds(q * 8 * ROWS + r, 8, stride=ROWS), :]
                pieces.append((x - take(mean, at, BY_ROW)) * take(scale, at, BY_ROW))
            feat = jnp.concatenate(pieces, axis=0).astype(jnp.bfloat16)
            kern = lax.dot_general(feat, feat, (((1,), (1,)), ((), ())), preferred_element_type=jnp.float32)
            part = jnp.sum((kern * kern).reshape(epochs // 8, 8, epochs), axis=0)
            square_ref[pl.ds(pl.multiple_of((b * ROWS + r) * 8, 8), 8), :] = part
            acc = kern if acc is None else acc + kern
        total_ref[...] += acc

    even = (x0_ref, sum0_ref, sq0_ref, mean0_ref, scale0_ref)
    odd = (x1_ref, sum1_ref, sq1_ref, mean1_ref, scale1_ref)
    blocks = block_len // ROWS

    correlate(0, even)

    def two_blocks(j, carry):
        b = 2 * j
        kernels(b, even)
        correlate(b + 1, odd)
        kernels(b + 1, odd)
        correlate(jnp.minimum(b + 2, blocks - 1), even)
        return carry

    lax.fori_loop(0, blocks // 2, two_blocks, 0)

    for half in range(block_len // LANES):
        sums = None
        for r in range(8):
            part = square_ref[pl.ds(half * LANES * 8 + r, LANES, stride=8), :]
            sums = part if sums is None else sums + part
        sums = jnp.sum(sums.T, axis=0, keepdims=True)
        spread_ref[half:half + 1, :] = jnp.sqrt(sums * (1.0 / (epochs * NB * NB)))
    exact = lax.Precision.HIGHEST
    half_way = jnp.dot(total_ref[...], perm_ref[...], precision=exact, preferred_element_type=jnp.float32)
    gram_ref[...] = jnp.dot(perm_ref[...].T, half_way, precision=exact, preferred_element_type=jnp.float32)


def sum_kernel(count, scale, part_ref, out_ref, took, send1, recv1, send2, recv2):
    me = lax.axis_index("bx")
    barrier = pltpu.get_barrier_semaphore()

    def greet(d, carry):
        pl.semaphore_signal(barrier, inc=1, device_id={"bx": lax.rem(me + d, count)}, device_id_type=MESH)
        return carry

    lax.fori_loop(1, count, greet, 0)
    pl.semaphore_wait(barrier, count - 1)

    def scatter(d):
        to = lax.rem(me + d, count)
        return pltpu.make_async_remote_copy(
            src_ref=part_ref.at[to], dst_ref=took.at[d], send_sem=send1.at[d], recv_sem=recv1.at[d],
            device_id={"bx": to}, device_id_type=MESH)

    def gather(d):
        return pltpu.make_async_remote_copy(
            src_ref=out_ref.at[me], dst_ref=out_ref.at[me], send_sem=send2.at[d], recv_sem=recv2.at[d],
            device_id={"bx": lax.rem(me + d, count)}, device_id_type=MESH)

    def landed(d):
        src = lax.rem(me + count - d, count)
        return pltpu.make_async_remote_copy(
            src_ref=out_ref.at[src], dst_ref=out_ref.at[src], send_sem=send2.at[d], recv_sem=recv2.at[d],
            device_id={"bx": lax.rem(me + d, count)}, device_id_type=MESH)

    def each(act):
        def body(d, carry):
            act(d)
            return carry
        lax.fori_loop(1, count, body, 0)

    each(lambda d: scatter(d).start())
    each(lambda d: scatter(d).wait_recv())

    def add(d, total):
        return total + took[d]

    out_ref[me] = lax.fori_loop(1, count, add, part_ref[me]) * scale
    each(lambda d: gather(d).start())
    each(lambda d: landed(d).wait_recv())
    each(lambda d: scatter(d).wait_send())
    each(lambda d: gather(d).wait_send())


def sum_over_bx(total, scale):
    count = lax.axis_size("bx")
    rows, cols = total.shape
    blocks = total.reshape(count, rows // count, cols)
    vmem = pl.BlockSpec(memory_space=pltpu.VMEM)
    return pl.pallas_call(
        functools.partial(sum_kernel, count, scale),
        in_specs=[vmem],
        out_specs=vmem,
        out_shape=jax.ShapeDtypeStruct(blocks.shape, jnp.float32),
        scratch_shapes=[pltpu.VMEM(blocks.shape, jnp.float32)] + [pltpu.SemaphoreType.DMA((count,))] * 4,
        compiler_params=pltpu.CompilerParams(collective_id=0, has_side_effects=True),
        name="sum_over_bx",
    )(blocks).reshape(rows, cols)


def per_device(bold, nbr_table, subject):
    epochs, points, block_len = bold.shape
    slots = nbr_table.shape[0]
    count = lax.axis_size("bx")
    bold = bold.transpose(1, 0, 2)
    left = lax.ppermute(bold[:, :, block_len - LEAD:], "bx", [(i, i + 1) for i in range(count - 1)])
    right = lax.ppermute(bold[:, :, :LEAD], "bx", [(i + 1, i) for i in range(count - 1)])
    vmem = pl.BlockSpec(memory_space=pltpu.VMEM)
    ext = jnp.concatenate([left, bold, right], axis=2)
    wide = ext.shape[2]
    groups = epochs // GROUP
    f32 = functools.partial(pltpu.VMEM, dtype=jnp.float32)
    spread, total = pl.pallas_call(
        features_kernel,
        in_specs=[vmem] * 3,
        out_specs=[vmem] * 2,
        out_shape=[jax.ShapeDtypeStruct((block_len // LANES, LANES), jnp.float32),
                   jax.ShapeDtypeStruct((epochs, epochs), jnp.float32)],
        scratch_shapes=[
            f32((points, epochs, wide)),
            pltpu.VMEM((2, points * epochs, SPAN + LANES), jnp.bfloat16),
            pltpu.VMEM((block_len // ROWS, groups, 2 * ROWS, LANES), jnp.bfloat16),
            pltpu.VMEM((block_len, slots), jnp.int32),
            pltpu.VMEM((block_len, slots), jnp.int32),
            f32((block_len, slots)),
            pltpu.VMEM((epochs, LANES), jnp.int32),
            f32((epochs, epochs)),
            *[f32((epochs * ROWS, LANES))] * 2,
            *[f32((epochs + 1, ROWS, LANES))] * 4,
            *[f32((SUBJ * ROWS, LANES))] * 4,
            f32((block_len * 8, epochs)),
            f32((epochs, epochs)),
        ],
        compiler_params=pltpu.CompilerParams(vmem_limit_bytes=60 * 1024 * 1024),
        name="features",
    )(ext, nbr_table, subject[None, :])
    gram_mean = sum_over_bx(total, 1.0 / (NB * block_len * count))
    return spread.reshape(block_len), gram_mean


def solution(mesh):
    return jax.shard_map(
        per_device,
        mesh=mesh,
        in_specs=(P("cohort", None, "bx"), P("cohort", "bx"), P("cohort")),
        out_specs=(P(("cohort", "bx")), P("cohort", None)),
        check_vma=False,
    )
```

time: 107 us -> 76.6 us (0.72)
  Pallas kernels: 89 us -> 63.2 us
  local copies, waits for them, and re-layouts: 7.59 us -> 4.57 us
  other arithmetic: 4.51 us -> 2.23 us
  waiting for transfers between devices: 0.01 us -> 1.15 us
    pallas_call x2 -> x1, Pallas kernels: 71.8 us -> 37.4 us  [per_device(): pl.pallas_call(features_kernel, in_specs=[vmem] * 3, out_specs=[vmem] * 2...]
    pallas_call x1, Pallas kernels: 17.2 us -> 25.8 us  [sum_over_bx(): pl.pallas_call(functools.partial(sum_kernel, count, scale), in_specs=[vme...]
    broadcast_in_dim x3 -> x0, local copies, waits for them, and re-layouts: 1.41 us -> none  [the longest x1 0.71 us: per_device(): sid = jnp.broadcast_to(subject[:, None], (epochs, LANES))]
    ppermute x1, waiting for transfers between devices: 0.01 us -> 1.14 us  [per_device(): lax.ppermute(bold[:, :, block_len - LEAD:], 'bx', [(i, i + 1) for i in ra...]
    reduce_sum x2 -> x0, other arithmetic: 1.13 us -> none  [the longest x1 1.01 us: per_device(): spread = jnp.sqrt(jnp.sum(squares, axis=1) / (epochs * NB * NB))]
  transfers between devices with their start and end apart: 2 -> 2, of which waited for: 0 -> 1; matrix products, arithmetic and copies ran while one was open for 2% -> 1% of each run, Pallas kernels for 11% -> 0%
where the time goes in v1:
time: 76.6 us; the launch traced here: 76.3 us
  Pallas kernels  63.2 us (83%)
  local copies, waits for them, and re-layouts  4.57 us (6%)
  starting transfers between devices  4.48 us (6%)
  other arithmetic  2.23 us (3%)
  waiting for transfers between devices  1.15 us (2%)
    pallas_call x1, Pallas kernels, per_device(): pl.pallas_call(features_kernel, in_specs=[vmem] * 3, out_specs=[vmem] * 2...  37.4 us
    pallas_call x1, Pallas kernels, sum_over_bx(): pl.pallas_call(functools.partial(sum_kernel, count, scale), in_specs=[vme...  25.8 us
    ppermute x1, starting transfers between devices, per_device(): lax.ppermute(bold[:, :, block_len - LEAD:], 'bx', [(i, i + 1) for i in ra...  3.06 us
    concatenate x1, other arithmetic, per_device(): ext = jnp.concatenate([left, bold, right], axis=2)  2.23 us
    slice x2, local copies, waits for them, and re-layouts, per_device(): bold[:, :, block_len - LEAD:]  2.18 us
  transfers between devices with their start and end apart: 2, of which 1 were waited for; matrix products, arithmetic and copies ran while one was open for 1% of the time, Pallas kernels for 0%

profile of v1, /device:TPU:0, one launch (start us, length us, event | category | flops | bytes accessed | tf_op | source)
XLA Modules:
  0.0 76.3 jit_solution(3701284572195098262)
XLA Ops:
  0.6 1.8 %fusion = (bf16[12,128,160]{2,1,0:T(8,128)(2,1)S(1)}, bf16[12,128,160]{2,1,0:T(8,128)(2,1)S(1)}) fusion(bf16[12,128,256]{2,1,0:T(8,128)(2,1)} %bitcast.5), kind=kLoop, calls=%fused_computation.1 | loop fusion | bytes 1966080 | tf_op jit(solution)/shard_map/slice | solution.py:259
  2.5 0.3 copy.6
  2.8 0.0 copy-start
  2.8 1.4 %collective-permute-start.1 = (bf16[12,128,160]{1,2,0:T(8,128)(2,1)S(1)}, bf16[12,128,160]{1,2,0:T(8,128)(2,1)S(1)}, u32[]{:S(2)}, u32[]{:S(2)}) collective-permute-start(bf16[12,128,160]{1,2,0:T(8,128)(2,1)S(1)} %copy.6), channel_id=1, source_target_pairs={{1,0},{2,1},{3,2},{4,3},{5,4},{6,5},{7,6},{8,7},{9,8},{10,9},{11,1... | collective-permute-start | bytes 1474568 | tf_op jit(solution)/shard_map/ppermute | solution.py:260
  4.3 0.3 copy.5
  4.6 3.1 %collective-permute-start = (bf16[12,128,160]{1,2,0:T(8,128)(2,1)S(1)}, bf16[12,128,160]{1,2,0:T(8,128)(2,1)S(1)}, u32[]{:S(2)}, u32[]{:S(2)}) collective-permute-start(bf16[12,128,160]{1,2,0:T(8,128)(2,1)S(1)} %copy.5), channel_id=1, source_target_pairs={{0,1},{1,2},{2,3},{3,4},{4,5},{5,6},{6,7},{7,8},{8,9},{9,10},{10,1... | collective-permute-start | bytes 1474568 | tf_op jit(solution)/shard_map/ppermute | solution.py:259
  7.7 0.0 collective-permute-done.1
  7.7 0.3 copy.8
  8.0 1.1 %collective-permute-done = bf16[12,128,160]{1,2,0:T(8,128)(2,1)S(1)} collective-permute-done((bf16[12,128,160]{1,2,0:T(8,128)(2,1)S(1)}, bf16[12,128,160]{1,2,0:T(8,128)(2,1)S(1)}, u32[]{:S(2)}, u32[]{:S(2)}) %collective-permute-start) | collective-permute-done | bytes 491552 | tf_op jit(solution)/shard_map/ppermute | solution.py:259
  9.1 0.3 copy.7
  9.4 0.0 copy-done
  9.4 2.2 %pad_maximum_fusion.ext_ref = bf16[12,128,576]{2,1,0:T(8,128)(2,1)} fusion(bf16[12,128,160]{2,1,0:T(8,128)(2,1)S(1)} %copy.8, bf16[12,128,256]{2,1,0:T(8,128)(2,1)S(1)} %bitcast.6, bf16[12,128,160]{2,1,0:T(8,128)(2,1)S(1)} %copy.7), kind=kLoop, calls=%fused_computation | loop fusion | flops 5308416 | bytes 3538944 | tf_op jit(solution)/shard_map/concatenate | solution.py:262
  11.6 37.4 %features.1 = (f32[2,128]{1,0:T(2,128)}, f32[128,128]{1,0:T(8,128)}) custom-call(bf16[12,128,576]{2,1,0:T(8,128)(2,1)} %pad_maximum_fusion.ext_ref, s32[128,256]{1,0:T(8,128)} %idx_ref.1, s32[1,128]{1,0:T(1,128)} %bitcast.9), custom_call_target="tpu_custom_call" | custom-call | tf_op jit(solution)/shard_map/features/pallas_call | solution.py:266
  49.0 25.8 %sum_over_bx.1 = f32[16,8,128]{2,1,0:T(8,128)} custom-call(f32[16,8,128]{2,1,0:T(8,128)} %bitcast.8), custom_call_target="tpu_custom_call" | custom-call | tf_op jit(solution)/shard_map/sum_over_bx/pallas_call | solution.py:243
  74.9 1.5 %copy.10 = f32[128,128]{1,0:T(8,128)} copy(f32[128,128]{1,0:T(8,128)} %bitcast.7) | data formatting | bytes 131072
Async XLA Ops:
  2.8 6.6 %copy-start = (bf16[128,12,256]{2,0,1:T(8,128)(2,1)S(1)}, bf16[128,12,256]{2,0,1:T(8,128)(2,1)}, u32[]{:S(2)}) copy-start(bf16[128,12,256]{2,0,1:T(8,128)(2,1)} %param.3) | copy-start | bytes 2359300
  2.8 4.9 %collective-permute-start.1 = (bf16[12,128,160]{1,2,0:T(8,128)(2,1)S(1)}, bf16[12,128,160]{1,2,0:T(8,128)(2,1)S(1)}, u32[]{:S(2)}, u32[]{:S(2)}) collective-permute-start(bf16[12,128,160]{1,2,0:T(8,128)(2,1)S(1)} %copy.6), channel_id=1, source_target_pairs={{1,0},{2,1},{3,2},{4,3},{5,4},{6,5},{7,6},{8,7},{9,8},{10,9},{11,1... | collective-permute-start | bytes 1474568 | tf_op jit(solution)/shard_map/ppermute | solution.py:260
  4.6 4.5 %collective-permute-start = (bf16[12,128,160]{1,2,0:T(8,128)(2,1)S(1)}, bf16[12,128,160]{1,2,0:T(8,128)(2,1)S(1)}, u32[]{:S(2)}, u32[]{:S(2)}) collective-permute-start(bf16[12,128,160]{1,2,0:T(8,128)(2,1)S(1)} %copy.5), channel_id=1, source_target_pairs={{0,1},{1,2},{2,3},{3,4},{4,5},{5,6},{6,7},{7,8},{8,9},{9,10},{10,1... | collective-permute-start | bytes 1474568 | tf_op jit(solution)/shard_map/ppermute | solution.py:259

commit v2 on v1

--- a/solution.py
+++ b/solution.py
@@ -37,16 +37,72 @@
     return centred * (1.0 / jnp.sqrt(jnp.sum(centred * centred, axis=0, keepdims=True) + 1.0))
 
 
-def features_kernel(ext_ref, idx_ref, subject_ref, spread_ref, gram_ref,
+def reduce_over_bx(count, scale, part_ref, out_ref, took, send1, recv1, send2, recv2):
+    me = lax.axis_index("bx")
+    rows = out_ref.shape[0] // count
+
+    def block(i):
+        return pl.ds(pl.multiple_of(i * rows, rows), rows)
+
+    def scatter(d):
+        to = lax.rem(me + d, count)
+        return pltpu.make_async_remote_copy(
+            src_ref=part_ref.at[block(to)], dst_ref=took.at[d], send_sem=send1.at[d], recv_sem=recv1.at[d],
+            device_id={"bx": to}, device_id_type=MESH)
+
+    def gather(d):
+        return pltpu.make_async_remote_copy(
+            src_ref=out_ref.at[block(me)], dst_ref=out_ref.at[block(me)], send_sem=send2.at[d], recv_sem=recv2.at[d],
+            device_id={"bx": lax.rem(me + d, count)}, device_id_type=MESH)
+
+    def landed(d):
+        src = lax.rem(me + count - d, count)
+        return pltpu.make_async_remote_copy(
+            src_ref=out_ref.at[block(src)], dst_ref=out_ref.at[block(src)], send_sem=send2.at[d], recv_sem=recv2.at[d],
+            device_id={"bx": lax.rem(me + d, count)}, device_id_type=MESH)
+
+    def each(act):
+        def body(d, carry):
+            act(d)
+            return carry
+        lax.fori_loop(1, count, body, 0)
+
+    each(lambda d: scatter(d).start())
+    each(lambda d: scatter(d).wait_recv())
+
+    def add(d, total):
+        return total + took[d]
+
+    out_ref[block(me), :] = lax.fori_loop(1, count, add, part_ref[block(me), :]) * scale
+    each(lambda d: gather(d).start())
+    each(lambda d: landed(d).wait_recv())
+    each(lambda d: scatter(d).wait_send())
+    each(lambda d: gather(d).wait_send())
+
+
+def greet_bx(count):
+    me = lax.axis_index("bx")
+    barrier = pltpu.get_barrier_semaphore()
+
+    def greet(d, carry):
+        pl.semaphore_signal(barrier, inc=1, device_id={"bx": lax.rem(me + d, count)}, device_id_type=MESH)
+        return carry
+
+    lax.fori_loop(1, count, greet, 0)
+
+
+def features_kernel(count, ext_ref, idx_ref, subject_ref, spread_ref, gram_ref,
                     sorted_ref, win_ref, own_ref, lane_ref, tile_ref, valid_ref, sid_ref, perm_ref,
                     x0_ref, x1_ref, sum0_ref, sum1_ref, sq0_ref, sq1_ref, mean0_ref, mean1_ref,
-                    scale0_ref, scale1_ref, square_ref, total_ref):
+                    scale0_ref, scale1_ref, square_ref, total_ref,
+                    took_ref, send1, recv1, send2, recv2):
     points, epochs, wide = ext_ref.shape
     slots, block_len = idx_ref.shape
     groups = epochs // GROUP
     depth = points * GROUP
     span = SPAN + LANES
 
+    greet_bx(count)
     named = jnp.broadcast_to(subject_ref[...], (epochs, LANES))
     named_t = named.T
     row = lax.broadcasted_iota(jnp.int32, (epochs, LANES), 0)
@@ -57,7 +113,8 @@
     perm_ref[...] = perm
     perm16 = perm.astype(jnp.bfloat16)
     one_row = subject_ref[...]
-    starts = [jnp.sum((one_row < s).astype(jnp.float32)).astype(jnp.int32) for s in range(SUBJ + 1)]
+    starts = [jnp.clip(jnp.sum((one_row < s).astype(jnp.float32)).astype(jnp.int32), 0, epochs)
+              for s in range(SUBJ + 1)]
     place = lax.broadcasted_iota(jnp.int32, (epochs, LANES), 0)
     sid = jnp.zeros((epochs, LANES), jnp.int32)
     for s in range(1, SUBJ):
@@ -134,6 +191,7 @@
                 squares = squares + x * x
                 sum_ref[i + 1] = running
                 sq_ref[i + 1] = squares
+            yield
 
     def kernels(b, refs):
         x_ref, sum_ref, sq_ref, mean_ref, scale_ref = refs
@@ -158,20 +216,30 @@
             part = jnp.sum((kern * kern).reshape(epochs // 8, 8, epochs), axis=0)
             square_ref[pl.ds(pl.multiple_of((b * ROWS + r) * 8, 8), 8), :] = part
             acc = kern if acc is None else acc + kern
+            yield
         total_ref[...] += acc
 
     even = (x0_ref, sum0_ref, sq0_ref, mean0_ref, scale0_ref)
     odd = (x1_ref, sum1_ref, sq1_ref, mean1_ref, scale1_ref)
     blocks = block_len // ROWS
 
-    correlate(0, even)
+    def together(first, second):
+        pace = groups // ROWS
+        for _ in range(ROWS):
+            for _ in range(pace):
+                next(first)
+            next(second)
+        for rest in (first, second):
+            for _ in rest:
+                pass
+
+    for _ in correlate(0, even):
+        pass
 
     def two_blocks(j, carry):
         b = 2 * j
-        kernels(b, even)
-        correlate(b + 1, odd)
-        kernels(b + 1, odd)
-        correlate(jnp.minimum(b + 2, blocks - 1), even)
+        together(correlate(b + 1, odd), kernels(b, even))
+        together(correlate(jnp.minimum(b + 2, blocks - 1), even), kernels(b + 1, odd))
         return carry
 
     lax.fori_loop(0, blocks // 2, two_blocks, 0)
@@ -185,70 +253,9 @@
         spread_ref[half:half + 1, :] = jnp.sqrt(sums * (1.0 / (epochs * NB * NB)))
     exact = lax.Precision.HIGHEST
     half_way = jnp.dot(total_ref[...], perm_ref[...], precision=exact, preferred_element_type=jnp.float32)
-    gram_ref[...] = jnp.dot(perm_ref[...].T, half_way, precision=exact, preferred_element_type=jnp.float32)
-
-
-def sum_kernel(count, scale, part_ref, out_ref, took, send1, recv1, send2, recv2):
-    me = lax.axis_index("bx")
-    barrier = pltpu.get_barrier_semaphore()
-
-    def greet(d, carry):
-        pl.semaphore_signal(barrier, inc=1, device_id={"bx": lax.rem(me + d, count)}, device_id_type=MESH)
-        return carry
-
-    lax.fori_loop(1, count, greet, 0)
-    pl.semaphore_wait(barrier, count - 1)
-
-    def scatter(d):
-        to = lax.rem(me + d, count)
-        return pltpu.make_async_remote_copy(
-            src_ref=part_ref.at[to], dst_ref=took.at[d], send_sem=send1.at[d], recv_sem=recv1.at[d],
-            device_id={"bx": to}, device_id_type=MESH)
-
-    def gather(d):
-        return pltpu.make_async_remote_copy(
-            src_ref=out_ref.at[me], dst_ref=out_ref.at[me], send_sem=send2.at[d], recv_sem=recv2.at[d],
-            device_id={"bx": lax.rem(me + d, count)}, device_id_type=MESH)
-
-    def landed(d):
-        src = lax.rem(me + count - d, count)
-        return pltpu.make_async_remote_copy(
-            src_ref=out_ref.at[src], dst_ref=out_ref.at[src], send_sem=send2.at[d], recv_sem=recv2.at[d],
-            device_id={"bx": lax.rem(me + d, count)}, device_id_type=MESH)
-
-    def each(act):
-        def body(d, carry):
-            act(d)
-            return carry
-        lax.fori_loop(1, count, body, 0)
-
-    each(lambda d: scatter(d).start())
-    each(lambda d: scatter(d).wait_recv())
-
-    def add(d, total):
-        return total + took[d]
-
-    out_ref[me] = lax.fori_loop(1, count, add, part_ref[me]) * scale
-    each(lambda d: gather(d).start())
-    each(lambda d: landed(d).wait_recv())
-    each(lambda d: scatter(d).wait_send())
-    each(lambda d: gather(d).wait_send())
-
-
-def sum_over_bx(total, scale):
-    count = lax.axis_size("bx")
-    rows, cols = total.shape
-    blocks = total.reshape(count, rows // count, cols)
-    vmem = pl.BlockSpec(memory_space=pltpu.VMEM)
-    return pl.pallas_call(
-        functools.partial(sum_kernel, count, scale),
-        in_specs=[vmem],
-        out_specs=vmem,
-        out_shape=jax.ShapeDtypeStruct(blocks.shape, jnp.float32),
-        scratch_shapes=[pltpu.VMEM(blocks.shape, jnp.float32)] + [pltpu.SemaphoreType.DMA((count,))] * 4,
-        compiler_params=pltpu.CompilerParams(collective_id=0, has_side_effects=True),
-        name="sum_over_bx",
-    )(blocks).reshape(rows, cols)
+    total_ref[...] = jnp.dot(perm_ref[...].T, half_way, precision=exact, preferred_element_type=jnp.float32)
+    pl.semaphore_wait(pltpu.get_barrier_semaphore(), count - 1)
+    reduce_over_bx(count, 1.0 / (NB * block_len * count), total_ref, gram_ref, took_ref, send1, recv1, send2, recv2)
 
 
 def per_device(bold, nbr_table, subject):
@@ -263,8 +270,8 @@
     wide = ext.shape[2]
     groups = epochs // GROUP
     f32 = functools.partial(pltpu.VMEM, dtype=jnp.float32)
-    spread, total = pl.pallas_call(
-        features_kernel,
+    spread, gram_mean = pl.pallas_call(
+        functools.partial(features_kernel, count),
         in_specs=[vmem] * 3,
         out_specs=[vmem] * 2,
         out_shape=[jax.ShapeDtypeStruct((block_len // LANES, LANES), jnp.float32),
@@ -283,11 +290,13 @@
             *[f32((SUBJ * ROWS, LANES))] * 4,
             f32((block_len * 8, epochs)),
             f32((epochs, epochs)),
+            f32((count, epochs // count, epochs)),
+            *[pltpu.SemaphoreType.DMA((count,))] * 4,
         ],
-        compiler_params=pltpu.CompilerParams(vmem_limit_bytes=60 * 1024 * 1024),
+        compiler_params=pltpu.CompilerParams(collective_id=0, has_side_effects=True,
+                                             vmem_limit_bytes=60 * 1024 * 1024),
         name="features",
     )(ext, nbr_table, subject[None, :])
-    gram_mean = sum_over_bx(total, 1.0 / (NB * block_len * count))
     return spread.reshape(block_len), gram_mean
 
 

time: 76.6 us -> 68.9 us (0.90)
  Pallas kernels: 63.2 us -> 54.2 us
  local copies, waits for them, and re-layouts: 4.57 us -> 5.8 us
    pallas_call x2 -> x1, Pallas kernels: 63.2 us -> 54.2 us  [per_device(): pl.pallas_call(functools.partial(features_kernel, count), in_specs=[vmem]...]
    unnamed x3 -> x4, local copies, waits for them, and re-layouts: 1.48 us -> 2.71 us
where the time goes in v2:
time: 68.9 us; the launch traced here: 68.6 us
  Pallas kernels  54.2 us (79%)
  local copies, waits for them, and re-layouts  5.8 us (8%)
  starting transfers between devices  4.48 us (7%)
  other arithmetic  2.23 us (3%)
  waiting for transfers between devices  1.15 us (2%)
  between operations  0.7 us (1%)
    pallas_call x1, Pallas kernels, per_device(): pl.pallas_call(functools.partial(features_kernel, count), in_specs=[vmem]...  54.2 us
    ppermute x1, starting transfers between devices, per_device(): lax.ppermute(bold[:, :, block_len - LEAD:], 'bx', [(i, i + 1) for i in ra...  3.06 us
    unnamed x4, local copies, waits for them, and re-layouts  2.71 us
    concatenate x1, other arithmetic, per_device(): ext = jnp.concatenate([left, bold, right], axis=2)  2.23 us
    slice x2, local copies, waits for them, and re-layouts, per_device(): bold[:, :, block_len - LEAD:]  2.18 us
    ppermute x1, starting transfers between devices, per_device(): lax.ppermute(bold[:, :, :LEAD], 'bx', [(i + 1, i) for i in range(count -...  1.42 us
  transfers between devices with their start and end apart: 2, of which 1 were waited for; matrix products, arithmetic and copies ran while one was open for 1% of the time, Pallas kernels for 0%

profile of v2, /device:TPU:0, one launch (start us, length us, event | category | flops | bytes accessed | tf_op | source)
XLA Modules:
  0.0 68.6 jit_solution(10809768983510542248)
XLA Ops:
  0.6 1.8 %fusion = (bf16[12,128,160]{2,1,0:T(8,128)(2,1)S(1)}, bf16[12,128,160]{2,1,0:T(8,128)(2,1)S(1)}) fusion(bf16[12,128,256]{2,1,0:T(8,128)(2,1)} %bitcast.3), kind=kLoop, calls=%fused_computation.1 | loop fusion | bytes 1966080 | tf_op jit(solution)/shard_map/slice | solution.py:266
  2.5 0.3 copy.6
  2.8 0.0 copy-start
  2.8 1.4 %collective-permute-start.1 = (bf16[12,128,160]{1,2,0:T(8,128)(2,1)S(1)}, bf16[12,128,160]{1,2,0:T(8,128)(2,1)S(1)}, u32[]{:S(2)}, u32[]{:S(2)}) collective-permute-start(bf16[12,128,160]{1,2,0:T(8,128)(2,1)S(1)} %copy.6), channel_id=1, source_target_pairs={{1,0},{2,1},{3,2},{4,3},{5,4},{6,5},{7,6},{8,7},{9,8},{10,9},{11,1... | collective-permute-start | bytes 1474568 | tf_op jit(solution)/shard_map/ppermute | solution.py:267
  4.3 0.3 copy.5
  4.6 3.1 %collective-permute-start = (bf16[12,128,160]{1,2,0:T(8,128)(2,1)S(1)}, bf16[12,128,160]{1,2,0:T(8,128)(2,1)S(1)}, u32[]{:S(2)}, u32[]{:S(2)}) collective-permute-start(bf16[12,128,160]{1,2,0:T(8,128)(2,1)S(1)} %copy.5), channel_id=1, source_target_pairs={{0,1},{1,2},{2,3},{3,4},{4,5},{5,6},{6,7},{7,8},{8,9},{9,10},{10,1... | collective-permute-start | bytes 1474568 | tf_op jit(solution)/shard_map/ppermute | solution.py:266
  7.7 0.0 collective-permute-done.1
  7.7 0.3 copy.8
  8.0 1.1 %collective-permute-done = bf16[12,128,160]{1,2,0:T(8,128)(2,1)S(1)} collective-permute-done((bf16[12,128,160]{1,2,0:T(8,128)(2,1)S(1)}, bf16[12,128,160]{1,2,0:T(8,128)(2,1)S(1)}, u32[]{:S(2)}, u32[]{:S(2)}) %collective-permute-start) | collective-permute-done | bytes 491552 | tf_op jit(solution)/shard_map/ppermute | solution.py:266
  9.1 0.3 copy.7
  9.4 0.0 copy-done
  9.4 2.2 %pad_maximum_fusion.ext_ref = bf16[12,128,576]{2,1,0:T(8,128)(2,1)} fusion(bf16[12,128,160]{2,1,0:T(8,128)(2,1)S(1)} %copy.8, bf16[12,128,256]{2,1,0:T(8,128)(2,1)S(1)} %bitcast.4, bf16[12,128,160]{2,1,0:T(8,128)(2,1)S(1)} %copy.7), kind=kLoop, calls=%fused_computation | loop fusion | flops 5308416 | bytes 3538944 | tf_op jit(solution)/shard_map/concatenate | solution.py:269
  11.6 54.2 %features.1 = (f32[2,128]{1,0:T(2,128)}, f32[128,128]{1,0:T(8,128)}) custom-call(bf16[12,128,576]{2,1,0:T(8,128)(2,1)} %pad_maximum_fusion.ext_ref, s32[128,256]{1,0:T(8,128)} %idx_ref.1, s32[1,128]{1,0:T(1,128)} %bitcast.6), custom_call_target="tpu_custom_call" | custom-call | tf_op jit(solution)/shard_map/features/pallas_call | solution.py:273
  65.9 1.2 %copy.11 = f32[256]{0:T(256)} copy(f32[256]{0:T(256)} %bitcast.5) | data formatting | bytes 2048
  67.1 1.5 %copy.12 = f32[128,128]{1,0:T(8,128)} copy(f32[128,128]{1,0:T(8,128)} %get-tuple-element.11) | data formatting | bytes 131072
Async XLA Ops:
  2.8 6.6 %copy-start = (bf16[128,12,256]{2,0,1:T(8,128)(2,1)S(1)}, bf16[128,12,256]{2,0,1:T(8,128)(2,1)}, u32[]{:S(2)}) copy-start(bf16[128,12,256]{2,0,1:T(8,128)(2,1)} %param.3) | copy-start | bytes 2359300
  2.8 4.9 %collective-permute-start.1 = (bf16[12,128,160]{1,2,0:T(8,128)(2,1)S(1)}, bf16[12,128,160]{1,2,0:T(8,128)(2,1)S(1)}, u32[]{:S(2)}, u32[]{:S(2)}) collective-permute-start(bf16[12,128,160]{1,2,0:T(8,128)(2,1)S(1)} %copy.6), channel_id=1, source_target_pairs={{1,0},{2,1},{3,2},{4,3},{5,4},{6,5},{7,6},{8,7},{9,8},{10,9},{11,1... | collective-permute-start | bytes 1474568 | tf_op jit(solution)/shard_map/ppermute | solution.py:267
  4.6 4.5 %collective-permute-start = (bf16[12,128,160]{1,2,0:T(8,128)(2,1)S(1)}, bf16[12,128,160]{1,2,0:T(8,128)(2,1)S(1)}, u32[]{:S(2)}, u32[]{:S(2)}) collective-permute-start(bf16[12,128,160]{1,2,0:T(8,128)(2,1)S(1)} %copy.5), channel_id=1, source_target_pairs={{0,1},{1,2},{2,3},{3,4},{4,5},{5,6},{6,7},{7,8},{8,9},{9,10},{10,1... | collective-permute-start | bytes 1474568 | tf_op jit(solution)/shard_map/ppermute | solution.py:266

commit v3 on v2

--- a/solution.py
+++ b/solution.py
@@ -15,9 +15,10 @@
 LANES = 128
 ROWS = 8
 GROUP = 8
-CHUNK = 64
-LEAD = 160
+AHEAD = 5
+HALF = 64
 SPAN = 384
+NEAR, FAR, EDGE = range(3)
 MESH = pl.DeviceIdType.MESH
 BY_ROW = lax.GatherDimensionNumbers(
     offset_dims=(), collapsed_slice_dims=(0,), start_index_map=(0,),
@@ -91,16 +92,40 @@
     lax.fori_loop(1, count, greet, 0)
 
 
-def features_kernel(count, ext_ref, idx_ref, subject_ref, spread_ref, gram_ref,
-                    sorted_ref, win_ref, own_ref, lane_ref, tile_ref, valid_ref, sid_ref, perm_ref,
-                    x0_ref, x1_ref, sum0_ref, sum1_ref, sq0_ref, sq1_ref, mean0_ref, mean1_ref,
-                    scale0_ref, scale1_ref, square_ref, total_ref,
-                    took_ref, send1, recv1, send2, recv2):
-    points, epochs, wide = ext_ref.shape
-    slots, block_len = idx_ref.shape
+def plan_blocks(block_len):
+    windows = ((NEAR, -HALF, 5 * LANES), (FAR, -LANES, 0), (FAR, 0, LANES),
+               (EDGE, -LANES - HALF, 4 * LANES), (EDGE, HALF, 6 * LANES))
+    left = list(range(block_len // ROWS))
+    runs = []
+    for phase, column, lane in windows:
+        fits = [b for b in left if column <= b * ROWS - REACH and b * ROWS + ROWS + REACH <= column + SPAN]
+        left = [b for b in left if b not in fits]
+        runs.append((phase, len(fits), fits[0], column, lane))
+        assert fits == list(range(fits[0], fits[0] + len(fits)))
+    assert not left and block_len == 2 * LANES
+    return runs
+
+
+def pick(value, runs):
+    result = runs[-1][1]
+    for bound, entry in runs[-2::-1]:
+        result = jnp.where(value < bound, entry, result)
+    return result
+
+
+def features_kernel(count, bold_ref, idx_ref, subject_ref, spread_ref, gram_ref,
+                    sorted_ref, win_ref, quarter_ref, halo_ref, own_ref, lane_ref, tile_ref, valid_ref,
+                    sid_ref, perm_ref, x0_ref, x1_ref, sum0_ref, sum1_ref, sq0_ref, sq1_ref,
+                    mean0_ref, mean1_ref, scale0_ref, scale1_ref, square_ref, total_ref, prod_ref,
+                    took_ref, send0, recv0, send1, recv1, send2, recv2):
+    points, epochs, block_len = bold_ref.shape
+    slots = idx_ref.shape[0]
     groups = epochs // GROUP
     depth = points * GROUP
-    span = SPAN + LANES
+    packed = points * epochs // 2
+    me = lax.axis_index("bx")
+    runs = plan_blocks(block_len)
+    ends = [sum(r[1] for r in runs[:i + 1]) for i in range(len(runs))]
 
     greet_bx(count)
     named = jnp.broadcast_to(subject_ref[...], (epochs, LANES))
@@ -112,46 +137,133 @@
     perm = (jnp.broadcast_to(rank, (epochs, LANES)) == row).astype(jnp.float32)
     perm_ref[...] = perm
     perm16 = perm.astype(jnp.bfloat16)
+
+    def arrange(t, carry):
+        sorted_ref[t] = jnp.dot(perm16, bold_ref[t], preferred_element_type=jnp.float32)
+        return carry
+
+    lax.fori_loop(0, points, arrange, 0)
+
+    blank = jnp.zeros((LANES - depth, block_len), jnp.float32)
+
+    def tile_of(i):
+        return slice(i * LANES, (i + 1) * LANES)
+
+    def join(low, high):
+        return jnp.concatenate([low, high], axis=1)
+
+    def turned(values):
+        return join(values[:, HALF:], values[:, :HALF])
+
+    def fill(g, carry):
+        cells = normalized(sorted_ref[:, pl.ds(pl.multiple_of(g * GROUP, GROUP), GROUP), :])
+        cells = cells.reshape(depth, block_len).astype(jnp.bfloat16)
+        rows = pl.ds(pl.multiple_of(g * depth, depth), depth)
+        here0, here1 = cells[:, :LANES], cells[:, LANES:]
+        turn0, turn1 = turned(here0), turned(here1)
+        win_ref[rows, tile_of(1)] = here0
+        win_ref[rows, tile_of(2)] = here1
+        win_ref[rows, tile_of(5)] = turn0
+        win_ref[rows, tile_of(6)] = join(turn0[:, :HALF], turn1[:, HALF:])
+        win_ref[rows, tile_of(7)] = turn1
+        return carry
+
+    lax.fori_loop(0, groups, fill, 0)
+
+    def pair_rows(g):
+        first = pl.multiple_of(g * depth, depth)
+        return pl.ds(first, depth), pl.ds(pl.multiple_of(first + packed, depth), depth)
+
+    def pack(g, carry):
+        upper, lower = pair_rows(g)
+        for q, straight in enumerate((1, None, 2, None)):
+            here, turn = ((1, 5), (1, 5), (2, 7), (2, 7))[q]
+            one, two = (here, turn) if straight else (turn, here)
+            quarter_ref[q, upper, :] = join(win_ref[upper, tile_of(one)][:, :HALF], win_ref[lower, tile_of(two)][:, HALF:])
+        return carry
+
+    lax.fori_loop(0, groups // 2, pack, 0)
+
+    pl.semaphore_wait(pltpu.get_barrier_semaphore(), count - 1)
+
+    def message(side, phase):
+        quarter = (3 - phase) if side == 0 else phase
+        to = me + 1 if side == 0 else me - 1
+        return pltpu.make_async_remote_copy(
+            src_ref=quarter_ref.at[quarter], dst_ref=halo_ref.at[side * 3 + phase],
+            send_sem=send0.at[side * 3 + phase], recv_sem=recv0.at[side * 3 + phase],
+            device_id={"bx": to}, device_id_type=MESH)
+
+    sends = (me < count - 1, me > 0)
+    gets = (me > 0, me < count - 1)
+    for phase in range(3):
+        for side in range(2):
+            @pl.when(sends[side])
+            def _():
+                message(side, phase).start()
+
+    for side in range(2):
+        @pl.when(jnp.logical_not(gets[side]))
+        def _():
+            for phase in range(3):
+                halo_ref[side * 3 + phase] = jnp.zeros((packed, LANES), jnp.bfloat16)
+
     one_row = subject_ref[...]
     starts = [jnp.clip(jnp.sum((one_row < s).astype(jnp.float32)).astype(jnp.int32), 0, epochs)
               for s in range(SUBJ + 1)]
-    place = lax.broadcasted_iota(jnp.int32, (epochs, LANES), 0)
     sid = jnp.zeros((epochs, LANES), jnp.int32)
     for s in range(1, SUBJ):
-        sid = sid + (place >= starts[s]).astype(jnp.int32)
+        sid = sid + (row >= starts[s]).astype(jnp.int32)
     sid_ref[...] = sid
 
-    def arrange(t, carry):
-        sorted_ref[t] = jnp.dot(perm16, ext_ref[t], preferred_element_type=jnp.float32)
-        return carry
-
-    lax.fori_loop(0, points, arrange, 0)
-
-    blank = jnp.zeros((LANES - depth, block_len), jnp.float32)
-
-    def fill(g, carry):
-        cells = normalized(sorted_ref[:, pl.ds(pl.multiple_of(g * GROUP, GROUP), GROUP), :])
-        cells = cells.reshape(depth, wide)
-        base = pl.multiple_of(g * depth, depth)
-        for side in range(2):
-            win_ref[side, pl.ds(base, depth), :] = cells[:, side * CHUNK:side * CHUNK + span].astype(jnp.bfloat16)
-        own = cells[:, LEAD:LEAD + block_len].astype(jnp.bfloat16).astype(jnp.float32)
+    def turn_own(g, carry):
+        rows = pl.ds(pl.multiple_of(g * depth, depth), depth)
+        own = win_ref[rows, LANES:LANES + block_len].astype(jnp.float32)
         flat = jnp.concatenate([own, blank], axis=0).T
         for b in range(block_len // ROWS):
             piece = flat[b * ROWS:(b + 1) * ROWS, :]
             own_ref[b, g] = jnp.concatenate([piece, piece], axis=0).astype(jnp.bfloat16)
         return carry
 
-    lax.fori_loop(0, groups, fill, 0)
+    lax.fori_loop(0, groups, turn_own, 0)
 
     for half in range(block_len // LANES):
         at = idx_ref[:, half * LANES:(half + 1) * LANES].T
         centre = lax.broadcasted_iota(jnp.int32, (LANES, slots), 0) + half * LANES
-        offset = at - (block_len - LEAD) - centre // CHUNK * CHUNK
+        column = pick(centre // ROWS, sorted((r[2] + r[1], r[3]) for r in runs))
+        offset = at - block_len - column
         part = slice(half * LANES, (half + 1) * LANES)
         valid_ref[part, :] = (at >= 0).astype(jnp.float32)
         lane_ref[part, :] = jnp.where(at >= 0, offset & (LANES - 1), 0)
         tile_ref[part, :] = jnp.where(at >= 0, offset >> 7, 0)
+
+    def arrived(phase):
+        for side in range(2):
+            @pl.when(gets[side])
+            def _():
+                message(side, phase).wait_recv()
+
+    def settle(phase):
+        arrived(phase)
+        left, right = halo_ref.at[phase], halo_ref.at[3 + phase]
+        inner_left, inner_right = (halo_ref.at[phase - 1], halo_ref.at[2 + phase]) if phase else (None, None)
+
+        def body(g, carry):
+            upper, lower = pair_rows(g)
+            near_l, near_r = left[upper, :], right[upper, :]
+            if phase == NEAR:
+                for rows, (l, r) in ((upper, (near_l, near_r[:, :HALF])), (lower, (near_l[:, HALF:], near_r[:, HALF:]))):
+                    win_ref[rows, tile_of(5)] = join(l[:, :HALF], win_ref[rows, tile_of(5)][:, HALF:])
+                    win_ref[rows, tile_of(7)] = join(win_ref[rows, tile_of(7)][:, :HALF], r)
+            else:
+                in_l, in_r = inner_left[upper, :], inner_right[upper, :]
+                a, b = (0, 3) if phase == FAR else (4, 8)
+                for rows, cut in ((upper, slice(0, HALF)), (lower, slice(HALF, LANES))):
+                    win_ref[rows, tile_of(a)] = join(near_l[:, cut], in_l[:, cut])
+                    win_ref[rows, tile_of(b)] = join(in_r[:, cut], near_r[:, cut])
+            return carry
+
+        lax.fori_loop(0, groups // 2, body, 0)
 
     total_ref[...] = jnp.zeros_like(total_ref)
     masks = []
@@ -164,10 +276,22 @@
         sum_ref[0] = jnp.zeros((ROWS, LANES), jnp.float32)
         sq_ref[0] = jnp.zeros((ROWS, LANES), jnp.float32)
 
-    def correlate(b, refs):
+    def nth(n):
+        n = jnp.asarray(n, jnp.int32)
+        block = n + pick(n, [(end, r[2] - (end - r[1])) for end, r in zip(ends, runs)])
+        lane = pick(n, [(end, r[4]) for end, r in zip(ends, runs)])
+        return block, pl.multiple_of(lane, LANES)
+
+    def product(at, g):
+        b, start = at
+        rhs = win_ref[g * depth:(g + 1) * depth, pl.ds(start, SPAN)]
+        own = own_ref[b, g]
+        lhs = jnp.concatenate([own * m for m in masks], axis=0)[:, :depth]
+        return jnp.dot(lhs, rhs, preferred_element_type=jnp.float32)
+
+    def correlate(at, refs, queue, after):
+        b = at[0]
         x_ref, sum_ref, sq_ref = refs[:3]
-        chunk = b // (CHUNK // ROWS)
-        start = pl.multiple_of((chunk // 2) * LANES, LANES)
         here = pl.ds(pl.multiple_of(b * ROWS, ROWS), ROWS)
         lane = lane_ref[here, :]
         tile = tile_ref[here, :]
@@ -176,10 +300,7 @@
         running = jnp.zeros((ROWS, LANES), jnp.float32)
         squares = jnp.zeros((ROWS, LANES), jnp.float32)
         for g in range(groups):
-            rhs = win_ref[lax.rem(chunk, 2), g * depth:(g + 1) * depth, pl.ds(start, SPAN)]
-            own = own_ref[b, g]
-            lhs = jnp.concatenate([own * m for m in masks], axis=0)[:, :depth]
-            prod = jnp.dot(lhs, rhs, preferred_element_type=jnp.float32)
+            prod = queue.pop(0)
             for e in range(GROUP):
                 r = e * ROWS
                 parts = [take(prod[r:r + ROWS, t * LANES:(t + 1) * LANES], lane, BY_LANE)
@@ -191,6 +312,8 @@
                 squares = squares + x * x
                 sum_ref[i + 1] = running
                 sq_ref[i + 1] = squares
+            ahead = g + AHEAD
+            queue.append(product(at, ahead) if ahead < groups else product(after, ahead - groups))
             yield
 
     def kernels(b, refs):
@@ -233,13 +356,34 @@
             for _ in rest:
                 pass
 
-    for _ in correlate(0, even):
+    def keep(queue):
+        for i, prod in enumerate(queue):
+            prod_ref[i] = prod
+
+    settle(NEAR)
+    queue = [product(nth(0), g) for g in range(AHEAD)]
+    for _ in correlate(nth(0), even, queue, nth(1)):
         pass
+    keep(queue)
+    near = sum(r[1] for r in runs if r[0] == NEAR)
+    outer = sum(r[1] for r in runs if r[0] == EDGE)
 
     def two_blocks(j, carry):
-        b = 2 * j
-        together(correlate(b + 1, odd), kernels(b, even))
-        together(correlate(jnp.minimum(b + 2, blocks - 1), even), kernels(b + 1, odd))
+        n = 2 * j
+
+        @pl.when(j == (near - 3) // 2 + 1)
+        def _():
+            settle(FAR)
+
+        @pl.when(j == (blocks - outer - 3) // 2 + 1)
+        def _():
+            settle(EDGE)
+
+        queue = [prod_ref[i] for i in range(AHEAD)]
+        last = nth(jnp.minimum(n + 2, blocks - 1))
+        together(correlate(nth(n + 1), odd, queue, last), kernels(nth(n)[0], even))
+        together(correlate(last, even, queue, nth(jnp.minimum(n + 3, blocks - 1))), kernels(nth(n + 1)[0], odd))
+        keep(queue)
         return carry
 
     lax.fori_loop(0, blocks // 2, two_blocks, 0)
@@ -254,7 +398,12 @@
     exact = lax.Precision.HIGHEST
     half_way = jnp.dot(total_ref[...], perm_ref[...], precision=exact, preferred_element_type=jnp.float32)
     total_ref[...] = jnp.dot(perm_ref[...].T, half_way, precision=exact, preferred_element_type=jnp.float32)
-    pl.semaphore_wait(pltpu.get_barrier_semaphore(), count - 1)
+    for phase in range(3):
+        for side in range(2):
+            @pl.when(sends[side])
+            def _():
+                message(side, phase).wait_send()
+
     reduce_over_bx(count, 1.0 / (NB * block_len * count), total_ref, gram_ref, took_ref, send1, recv1, send2, recv2)
 
 
@@ -263,11 +412,7 @@
     slots = nbr_table.shape[0]
     count = lax.axis_size("bx")
     bold = bold.transpose(1, 0, 2)
-    left = lax.ppermute(bold[:, :, block_len - LEAD:], "bx", [(i, i + 1) for i in range(count - 1)])
-    right = lax.ppermute(bold[:, :, :LEAD], "bx", [(i + 1, i) for i in range(count - 1)])
     vmem = pl.BlockSpec(memory_space=pltpu.VMEM)
-    ext = jnp.concatenate([left, bold, right], axis=2)
-    wide = ext.shape[2]
     groups = epochs // GROUP
     f32 = functools.partial(pltpu.VMEM, dtype=jnp.float32)
     spread, gram_mean = pl.pallas_call(
@@ -277,8 +422,10 @@
         out_shape=[jax.ShapeDtypeStruct((block_len // LANES, LANES), jnp.float32),
                    jax.ShapeDtypeStruct((epochs, epochs), jnp.float32)],
         scratch_shapes=[
-            f32((points, epochs, wide)),
-            pltpu.VMEM((2, points * epochs, SPAN + LANES), jnp.bfloat16),
+            f32((points, epochs, block_len)),
+            pltpu.VMEM((points * epochs, 9 * LANES), jnp.bfloat16),
+            pltpu.VMEM((4, points * epochs // 2, LANES), jnp.bfloat16),
+            pltpu.VMEM((6, points * epochs // 2, LANES), jnp.bfloat16),
             pltpu.VMEM((block_len // ROWS, groups, 2 * ROWS, LANES), jnp.bfloat16),
             pltpu.VMEM((block_len, slots), jnp.int32),
             pltpu.VMEM((block_len, slots), jnp.int32),
@@ -290,13 +437,15 @@
             *[f32((SUBJ * ROWS, LANES))] * 4,
             f32((block_len * 8, epochs)),
             f32((epochs, epochs)),
+            f32((AHEAD, GROUP * ROWS, SPAN)),
             f32((count, epochs // count, epochs)),
+            *[pltpu.SemaphoreType.DMA((6,))] * 2,
             *[pltpu.SemaphoreType.DMA((count,))] * 4,
         ],
         compiler_params=pltpu.CompilerParams(collective_id=0, has_side_effects=True,
                                              vmem_limit_bytes=60 * 1024 * 1024),
         name="features",
-    )(ext, nbr_table, subject[None, :])
+    )(bold, nbr_table, subject[None, :])
     return spread.reshape(block_len), gram_mean
 
 

time: 68.9 us -> 53.5 us (0.78)
  starting transfers between devices: 4.48 us -> 0 us
  Pallas kernels: 54.2 us -> 50 us
  local copies, waits for them, and re-layouts: 5.8 us -> 2.69 us
  other arithmetic: 2.23 us -> 0 us
  waiting for transfers between devices: 1.15 us -> 0 us
    ppermute x2 -> x0, starting transfers between devices: 4.48 us -> none  [the longest x1 3.06 us: per_device(): lax.ppermute(bold[:, :, block_len - LEAD:], 'bx', [(i, i + 1) for i in ra...]
    pallas_call x1, Pallas kernels: 54.2 us -> 50 us  [per_device(): pl.pallas_call(functools.partial(features_kernel, count), in_specs=[vmem]...]
    slice x3 -> x0, local copies, waits for them, and re-layouts: 2.53 us -> none  [the longest x2 2.18 us: per_device(): bold[:, :, block_len - LEAD:]]
    concatenate x1 -> x0, other arithmetic: 2.23 us -> none  [per_device(): ext = jnp.concatenate([left, bold, right], axis=2)]
    ppermute x2 -> x0, waiting for transfers between devices: 1.15 us -> none  [the longest x1 1.14 us: per_device(): lax.ppermute(bold[:, :, block_len - LEAD:], 'bx', [(i, i + 1) for i in ra...]
  transfers between devices with their start and end apart: 2 -> 0, of which waited for: 1 -> 0; matrix products, arithmetic and copies ran while one was open for 1% -> 0% of each run, Pallas kernels for 0% -> 0%
where the time goes in v3:
time: 53.5 us; the launch traced here: 53.3 us
  Pallas kernels  50 us (93%)
  local copies, waits for them, and re-layouts  2.69 us (5%)
  between operations  0.65 us (1%)
    pallas_call x1, Pallas kernels, per_device(): pl.pallas_call(functools.partial(features_kernel, count), in_specs=[vmem]...  50 us
    unnamed x4, local copies, waits for them, and re-layouts  2.69 us

profile of v3, /device:TPU:0, one launch (start us, length us, event | category | flops | bytes accessed | tf_op | source)
XLA Modules:
  0.0 53.3 jit_solution(15445970382257934928)
XLA Ops:
  0.6 50.0 %features.1 = (f32[2,128]{1,0:T(2,128)}, f32[128,128]{1,0:T(8,128)}) custom-call(bf16[12,128,256]{2,1,0:T(8,128)(2,1)} %bitcast.3, s32[128,256]{1,0:T(8,128)} %idx_ref.1, s32[1,128]{1,0:T(1,128)} %bitcast.5), custom_call_target="tpu_custom_call" | custom-call | tf_op jit(solution)/shard_map/features/pallas_call | solution.py:418
  50.6 0.0 copy-start
  50.6 0.7 %copy-done = f32[2,128]{1,0:T(2,128)S(1)} copy-done((f32[2,128]{1,0:T(2,128)S(1)}, f32[2,128]{1,0:T(2,128)}, u32[]{:S(2)}) %copy-start) | copy-done | bytes 1048
  51.3 0.6 %copy.7 = f32[256]{0:T(256)} copy(f32[256]{0:T(256)S(1)} %bitcast.4) | data formatting | bytes 2048
  51.8 1.5 %copy.8 = f32[128,128]{1,0:T(8,128)} copy(f32[128,128]{1,0:T(8,128)} %get-tuple-element.9) | data formatting | bytes 131072
Async XLA Ops:
  50.6 0.7 %copy-start = (f32[2,128]{1,0:T(2,128)S(1)}, f32[2,128]{1,0:T(2,128)}, u32[]{:S(2)}) copy-start(f32[2,128]{1,0:T(2,128)} %get-tuple-element.4) | copy-start | bytes 3076

commit v4 on v3

--- a/solution.py
+++ b/solution.py
@@ -38,9 +38,9 @@
     return centred * (1.0 / jnp.sqrt(jnp.sum(centred * centred, axis=0, keepdims=True) + 1.0))
 
 
-def reduce_over_bx(count, scale, part_ref, out_ref, took, send1, recv1, send2, recv2):
+def reduce_over_bx(count, scale, between, part_ref, out_ref, took, send1, recv1, send2, recv2):
     me = lax.axis_index("bx")
-    rows = out_ref.shape[0] // count
+    rows = part_ref.shape[0] // count
 
     def block(i):
         return pl.ds(pl.multiple_of(i * rows, rows), rows)
@@ -66,9 +66,14 @@
         def body(d, carry):
             act(d)
             return carry
-        lax.fori_loop(1, count, body, 0)
+        if count <= 16:
+            for d in range(1, count):
+                act(d)
+        else:
+            lax.fori_loop(1, count, body, 0)
 
     each(lambda d: scatter(d).start())
+    between()
     each(lambda d: scatter(d).wait_recv())
 
     def add(d, total):
@@ -76,8 +81,8 @@
 
     out_ref[block(me), :] = lax.fori_loop(1, count, add, part_ref[block(me), :]) * scale
     each(lambda d: gather(d).start())
+    each(lambda d: scatter(d).wait_send())
     each(lambda d: landed(d).wait_recv())
-    each(lambda d: scatter(d).wait_send())
     each(lambda d: gather(d).wait_send())
 
 
@@ -113,11 +118,19 @@
     return result
 
 
-def features_kernel(count, bold_ref, idx_ref, subject_ref, spread_ref, gram_ref,
+def fourfold(body):
+    def step(i, carry):
+        for k in range(4):
+            carry = body(4 * i + k, carry)
+        return carry
+    return step
+
+
+def features_kernel(count, bold_hbm, idx_hbm, subject_hbm, out_ref,
                     sorted_ref, win_ref, quarter_ref, halo_ref, own_ref, lane_ref, tile_ref, valid_ref,
                     sid_ref, perm_ref, x0_ref, x1_ref, sum0_ref, sum1_ref, sq0_ref, sq1_ref,
                     mean0_ref, mean1_ref, scale0_ref, scale1_ref, square_ref, total_ref, prod_ref,
-                    took_ref, send0, recv0, send1, recv1, send2, recv2):
+                    bold_ref, idx_ref, subject_ref, load_sem, took_ref, send0, recv0, send1, recv1, send2, recv2):
     points, epochs, block_len = bold_ref.shape
     slots = idx_ref.shape[0]
     groups = epochs // GROUP
@@ -127,7 +140,12 @@
     runs = plan_blocks(block_len)
     ends = [sum(r[1] for r in runs[:i + 1]) for i in range(len(runs))]
 
+    loads = [pltpu.make_async_copy(src, dst, load_sem.at[i]) for i, (src, dst) in enumerate(
+        ((subject_hbm, subject_ref), (bold_hbm, bold_ref), (idx_hbm, idx_ref)))]
+    for load in loads:
+        load.start()
     greet_bx(count)
+    loads[0].wait()
     named = jnp.broadcast_to(subject_ref[...], (epochs, LANES))
     named_t = named.T
     row = lax.broadcasted_iota(jnp.int32, (epochs, LANES), 0)
@@ -138,11 +156,13 @@
     perm_ref[...] = perm
     perm16 = perm.astype(jnp.bfloat16)
 
+    loads[1].wait()
+
     def arrange(t, carry):
         sorted_ref[t] = jnp.dot(perm16, bold_ref[t], preferred_element_type=jnp.float32)
         return carry
 
-    lax.fori_loop(0, points, arrange, 0)
+    lax.fori_loop(0, points // 4, fourfold(arrange), 0)
 
     blank = jnp.zeros((LANES - depth, block_len), jnp.float32)
 
@@ -168,22 +188,24 @@
         win_ref[rows, tile_of(7)] = turn1
         return carry
 
-    lax.fori_loop(0, groups, fill, 0)
+    lax.fori_loop(0, groups // 4, fourfold(fill), 0)
 
     def pair_rows(g):
         first = pl.multiple_of(g * depth, depth)
         return pl.ds(first, depth), pl.ds(pl.multiple_of(first + packed, depth), depth)
 
-    def pack(g, carry):
-        upper, lower = pair_rows(g)
-        for q, straight in enumerate((1, None, 2, None)):
-            here, turn = ((1, 5), (1, 5), (2, 7), (2, 7))[q]
-            one, two = (here, turn) if straight else (turn, here)
-            quarter_ref[q, upper, :] = join(win_ref[upper, tile_of(one)][:, :HALF], win_ref[lower, tile_of(two)][:, HALF:])
-        return carry
-
-    lax.fori_loop(0, groups // 2, pack, 0)
-
+    def pack(quarters):
+        def body(g, carry):
+            upper, lower = pair_rows(g)
+            for q in quarters:
+                one, two = ((1, 5), (5, 1), (2, 7), (7, 2))[q]
+                quarter_ref[q, upper, :] = join(
+                    win_ref[upper, tile_of(one)][:, :HALF], win_ref[lower, tile_of(two)][:, HALF:])
+            return carry
+
+        lax.fori_loop(0, groups // 8, fourfold(body), 0)
+
+    pack((0, 3))
     pl.semaphore_wait(pltpu.get_barrier_semaphore(), count - 1)
 
     def message(side, phase):
@@ -196,11 +218,14 @@
 
     sends = (me < count - 1, me > 0)
     gets = (me > 0, me < count - 1)
-    for phase in range(3):
+    def send(phase):
         for side in range(2):
             @pl.when(sends[side])
             def _():
                 message(side, phase).start()
+
+    send(NEAR)
+    pack((1, 2))
 
     for side in range(2):
         @pl.when(jnp.logical_not(gets[side]))
@@ -225,8 +250,9 @@
             own_ref[b, g] = jnp.concatenate([piece, piece], axis=0).astype(jnp.bfloat16)
         return carry
 
-    lax.fori_loop(0, groups, turn_own, 0)
-
+    lax.fori_loop(0, groups // 4, fourfold(turn_own), 0)
+
+    loads[2].wait()
     for half in range(block_len // LANES):
         at = idx_ref[:, half * LANES:(half + 1) * LANES].T
         centre = lax.broadcasted_iota(jnp.int32, (LANES, slots), 0) + half * LANES
@@ -245,6 +271,8 @@
 
     def settle(phase):
         arrived(phase)
+        if phase != EDGE:
+            send(phase + 1)
         left, right = halo_ref.at[phase], halo_ref.at[3 + phase]
         inner_left, inner_right = (halo_ref.at[phase - 1], halo_ref.at[2 + phase]) if phase else (None, None)
 
@@ -263,7 +291,7 @@
                     win_ref[rows, tile_of(b)] = join(in_r[:, cut], near_r[:, cut])
             return carry
 
-        lax.fori_loop(0, groups // 2, body, 0)
+        lax.fori_loop(0, groups // 8, fourfold(body), 0)
 
     total_ref[...] = jnp.zeros_like(total_ref)
     masks = []
@@ -313,7 +341,10 @@
                 sum_ref[i + 1] = running
                 sq_ref[i + 1] = squares
             ahead = g + AHEAD
-            queue.append(product(at, ahead) if ahead < groups else product(after, ahead - groups))
+            if ahead < groups:
+                queue.append(product(at, ahead))
+            elif after is not None:
+                queue.append(product(after, ahead - groups))
             yield
 
     def kernels(b, refs):
@@ -380,21 +411,18 @@
             settle(EDGE)
 
         queue = [prod_ref[i] for i in range(AHEAD)]
-        last = nth(jnp.minimum(n + 2, blocks - 1))
+        last = nth(n + 2)
         together(correlate(nth(n + 1), odd, queue, last), kernels(nth(n)[0], even))
-        together(correlate(last, even, queue, nth(jnp.minimum(n + 3, blocks - 1))), kernels(nth(n + 1)[0], odd))
+        together(correlate(last, even, queue, nth(n + 3)), kernels(nth(n + 1)[0], odd))
         keep(queue)
         return carry
 
-    lax.fori_loop(0, blocks // 2, two_blocks, 0)
-
-    for half in range(block_len // LANES):
-        sums = None
-        for r in range(8):
-            part = square_ref[pl.ds(half * LANES * 8 + r, LANES, stride=8), :]
-            sums = part if sums is None else sums + part
-        sums = jnp.sum(sums.T, axis=0, keepdims=True)
-        spread_ref[half:half + 1, :] = jnp.sqrt(sums * (1.0 / (epochs * NB * NB)))
+    lax.fori_loop(0, blocks // 2 - 1, two_blocks, 0)
+    queue = [prod_ref[i] for i in range(AHEAD)]
+    together(correlate(nth(blocks - 1), odd, queue, None), kernels(nth(blocks - 2)[0], even))
+    for _ in kernels(nth(blocks - 1)[0], odd):
+        pass
+
     exact = lax.Precision.HIGHEST
     half_way = jnp.dot(total_ref[...], perm_ref[...], precision=exact, preferred_element_type=jnp.float32)
     total_ref[...] = jnp.dot(perm_ref[...].T, half_way, precision=exact, preferred_element_type=jnp.float32)
@@ -404,7 +432,16 @@
             def _():
                 message(side, phase).wait_send()
 
-    reduce_over_bx(count, 1.0 / (NB * block_len * count), total_ref, gram_ref, took_ref, send1, recv1, send2, recv2)
+    def spreads():
+        for half in range(block_len // LANES):
+            sums = None
+            for r in range(8):
+                part = square_ref[pl.ds(half * LANES * 8 + r, LANES, stride=8), :]
+                sums = part if sums is None else sums + part
+            sums = jnp.sum(sums.T, axis=0, keepdims=True)
+            out_ref[epochs + half:epochs + half + 1, :] = jnp.sqrt(sums * (1.0 / (epochs * NB * NB)))
+
+    reduce_over_bx(count, 1.0 / (NB * block_len * count), spreads, total_ref, out_ref, took_ref, send1, recv1, send2, recv2)
 
 
 def per_device(bold, nbr_table, subject):
@@ -415,12 +452,11 @@
     vmem = pl.BlockSpec(memory_space=pltpu.VMEM)
     groups = epochs // GROUP
     f32 = functools.partial(pltpu.VMEM, dtype=jnp.float32)
-    spread, gram_mean = pl.pallas_call(
+    packed = pl.pallas_call(
         functools.partial(features_kernel, count),
-        in_specs=[vmem] * 3,
-        out_specs=[vmem] * 2,
-        out_shape=[jax.ShapeDtypeStruct((block_len // LANES, LANES), jnp.float32),
-                   jax.ShapeDtypeStruct((epochs, epochs), jnp.float32)],
+        in_specs=[pl.BlockSpec(memory_space=pl.ANY)] * 3,
+        out_specs=vmem,
+        out_shape=jax.ShapeDtypeStruct((epochs + ROWS, epochs), jnp.float32),
         scratch_shapes=[
             f32((points, epochs, block_len)),
             pltpu.VMEM((points * epochs, 9 * LANES), jnp.bfloat16),
@@ -438,6 +474,10 @@
             f32((block_len * 8, epochs)),
             f32((epochs, epochs)),
             f32((AHEAD, GROUP * ROWS, SPAN)),
+            pltpu.VMEM((points, epochs, block_len), jnp.bfloat16),
+            pltpu.VMEM((slots, block_len), jnp.int32),
+            pltpu.VMEM((1, epochs), jnp.int32),
+            pltpu.SemaphoreType.DMA((3,)),
             f32((count, epochs // count, epochs)),
             *[pltpu.SemaphoreType.DMA((6,))] * 2,
             *[pltpu.SemaphoreType.DMA((count,))] * 4,
@@ -446,7 +486,8 @@
                                              vmem_limit_bytes=60 * 1024 * 1024),
         name="features",
     )(bold, nbr_table, subject[None, :])
-    return spread.reshape(block_len), gram_mean
+    spread = packed[epochs:epochs + block_len // LANES].reshape(block_len)
+    return spread, packed[:epochs]
 
 
 def solution(mesh):

time: 53.5 us -> 46.5 us (0.87)
  Pallas kernels: 50 us -> 42.9 us
    pallas_call x1, Pallas kernels: 50 us -> 42.9 us  [per_device(): pl.pallas_call(functools.partial(features_kernel, count), in_specs=[pl.Bl...]
    unnamed x4 -> x0, local copies, waits for them, and re-layouts: 2.69 us -> none
    slice x0 -> x1, local copies, waits for them, and re-layouts: none -> 1.47 us  [per_device(): return (spread, packed[:epochs])]
    reshape x0 -> x1, local copies, waits for them, and re-layouts: none -> 1.24 us  [per_device(): spread = packed[epochs:epochs + block_len // LANES].reshape(block_len)]
where the time goes in v4:
time: 46.5 us; the launch traced here: 46.3 us
  Pallas kernels  42.9 us (92%)
  local copies, waits for them, and re-layouts  2.71 us (6%)
  between operations  0.64 us (1%)
    pallas_call x1, Pallas kernels, per_device(): pl.pallas_call(functools.partial(features_kernel, count), in_specs=[pl.Bl...  42.9 us
    slice x1, local copies, waits for them, and re-layouts, per_device(): return (spread, packed[:epochs])  1.47 us
    reshape x1, local copies, waits for them, and re-layouts, per_device(): spread = packed[epochs:epochs + block_len // LANES].reshape(block_len)  1.24 us

profile of v4, /device:TPU:0, one launch (start us, length us, event | category | flops | bytes accessed | tf_op | source)
XLA Modules:
  0.0 46.3 jit_solution(5336032311182342485)
XLA Ops:
  0.6 42.9 %features.1 = f32[136,128]{1,0:T(8,128)} custom-call(bf16[12,128,256]{2,1,0:T(8,128)(2,1)} %bitcast.4, s32[128,256]{1,0:T(8,128)} %idx_hbm.1, s32[1,128]{1,0:T(1,128)} %bitcast.5), custom_call_target="tpu_custom_call" | custom-call | tf_op jit(solution)/shard_map/features/pallas_call | solution.py:455
  43.6 1.2 %slice_bitcast_fusion = f32[256]{0:T(256)} fusion(f32[136,128]{1,0:T(8,128)} %features.1), kind=kLoop, calls=%fused_computation | loop fusion | bytes 2048 | tf_op jit(solution)/shard_map/reshape | solution.py:489
  44.8 1.5 %slice.7 = f32[128,128]{1,0:T(8,128)} slice(f32[136,128]{1,0:T(8,128)} %features.1), slice={[0:128], [0:128]} | slice | bytes 131072 | tf_op jit(solution)/shard_map/slice | solution.py:490
